TPU v7x, 256 devices: a whole 4x4x8 slice. The times are simulated.
256 devices in a mesh: dp: 32 (over x, z_lo, core), head: 8 (over y, z_hi).
Axes of the slice: x: 4, y: 4, z: 8 (z_hi: 2, z_lo: 4; z = z_hi * 4 + z_lo), core: 2. Of those that a mesh axis runs over, the one named last changes fastest.
Arguments:
- frames_in: bfloat16 [32, 8, 320, 640], P('dp', 'head'), may hold values from -6 to 6
- ln1_gain: float32 [1280], replicated, may hold values from 0.25 to 1.75
- ln1_bias: float32 [1280], replicated, may hold values from -3 to 3
- qkv_weight: bfloat16 [1280, 3, 1024], P('dp', None, 'head'), may hold values from -0.1875 to 0.1875
- qv_bias: float32 [2, 1024], P(None, 'head'), may hold values from -3 to 3
- out_weight: bfloat16 [1024, 1280], P(('head', 'dp')), may hold values from -0.1875 to 0.1875
- out_bias: float32 [1280], P('head'), may hold values from -3 to 3
- ln2_gain: float32 [1280], replicated, may hold values from 0.25 to 1.75
- ln2_bias: float32 [1280], replicated, may hold values from -3 to 3
- fc1_weight: bfloat16 [1280, 5120], P('dp', 'head'), may hold values from -0.15625 to 0.15625
- fc1_bias: float32 [5120], P('head'), may hold values from -3 to 3
- fc2_weight: bfloat16 [5120, 1280], P(('head', 'dp')), may hold values from -0.078125 to 0.078125
- fc2_bias: float32 [1280], P('head'), may hold values from -3 to 3
- server_of_clip: int32 [32], replicated, may hold values from 0 to 7
Outputs:
- encoded: bfloat16 [32, 8, 320, 640], P('dp', 'head')
All inputs are finite; a program needn't handle non-finite values.
Results may differ from a plain program's by a relative error of at most 0.014.
Values may be sent and summed in bfloat16 or wider, within the bound.
A program may use at most 64 MiB of HBM per device.

v0:
```python
import jax
import jax.numpy as jnp
from jax import lax
from jax.sharding import Mesh
from jax.sharding import PartitionSpec as P

HDIM = 64
HEAD = ("head_0", "head_1")
HEAD_DP = ("head_0", "head_1", "dp")


epsilon = 1e-05


def laid_out(blocks, dim):
    dims = list(blocks.shape[1:])
    dims[dim] *= blocks.shape[0]
    return jnp.moveaxis(blocks, 0, dim).reshape(dims)


def sent_to_all(value, axis):
    copies = jnp.broadcast_to(value, (lax.axis_size(axis), *value.shape))
    return lax.all_to_all(copies, axis, split_axis=0, concat_axis=0, tiled=True)


def gather_directly(value, axis, dim):
    return laid_out(sent_to_all(value, axis), dim)


def own_rows(terms, axes):
    total = terms.astype(jnp.bfloat16)
    for axis in axes:
        total = lax.psum_scatter(total, axis, scatter_dimension=0, tiled=True)
    return total.astype(jnp.float32)


def layer_norm(matrix, gain_row, shift_row):
    floats = matrix.astype(jnp.float32)
    center = jnp.mean(floats, axis=-1, keepdims=True)
    spread = jnp.mean(jnp.square(floats - center), axis=-1, keepdims=True)
    return ((floats - center) * lax.rsqrt(spread + epsilon) * gain_row + shift_row).astype(
        jnp.bfloat16
    )


def normalize(residual_in, gain_row, shift_row):
    whole_rows = lax.all_gather(residual_in, HEAD, axis=1, tiled=True)
    return layer_norm(whole_rows, gain_row, shift_row)


def attend(queries, key_rows, value_rows):

    def single(triple):
        query_head, key_head, value_head = triple
        scores = jnp.dot(query_head, key_head.T, preferred_element_type=jnp.float32)
        maxima = jnp.max(scores, axis=-1, keepdims=True)
        weights = jnp.exp(scores - maxima)
        probability = (weights / jnp.sum(weights, axis=-1, keepdims=True)).astype(jnp.bfloat16)
        return jnp.dot(probability, value_head, preferred_element_type=jnp.float32).astype(
            jnp.bfloat16
        )

    per_head = lax.map(
        single,
        (jnp.swapaxes(queries, 0, 1), jnp.swapaxes(key_rows, 0, 1), jnp.swapaxes(value_rows, 0, 1)),
    )
    return jnp.swapaxes(per_head, 0, 1).reshape(queries.shape[0], -1)


def slot_order(server_list):
    clip_count = server_list.shape[0]
    indices = jnp.arange(clip_count, dtype=jnp.int32)
    earlier = (server_list[None, :] < server_list[:, None]) | (
        server_list[None, :] == server_list[:, None]
    ) & (indices[None, :] < indices[:, None])
    slot_of = jnp.sum(earlier.astype(jnp.int32), axis=1)
    return jnp.sum(jnp.where(slot_of[None, :] == indices[:, None], indices[None, :], 0), axis=1)


def regroup(block_rows, clip_order):
    group_size = lax.axis_size("dp")
    piece_rows = block_rows.reshape(group_size, -1)
    shuffled = lax.all_to_all(piece_rows, "dp", split_axis=0, concat_axis=0, tiled=True)
    picked = jnp.take(shuffled, clip_order, axis=0)
    returned = lax.all_to_all(picked, "dp", split_axis=0, concat_axis=0, tiled=True)
    return returned.reshape(block_rows.shape)


def block_term(operand, weight_rows, row_count, frame_count, local_width):
    blocks = row_count // frame_count
    product = jnp.dot(operand, weight_rows, preferred_element_type=jnp.float32)
    return (
        product.reshape(frame_count, blocks, local_width)
        .transpose(1, 0, 2)
        .reshape(blocks * frame_count, local_width)
    )


def on_device(
    frames_in,
    ln1_gain,
    ln1_bias,
    qkv_weight,
    qv_bias,
    out_weight,
    out_bias,
    ln2_gain,
    ln2_bias,
    fc1_weight,
    fc1_bias,
    fc2_weight,
    fc2_bias,
    server_of_clip,
):
    clip_order = slot_order(server_of_clip)
    group_rows = frames_in.shape[2]
    local_width = frames_in.shape[3] // 4
    frame_count = group_rows * 4
    residual_in = frames_in[0, 0].reshape(frame_count, local_width)
    residual_in = regroup(residual_in, clip_order)
    head_count = lax.axis_size(HEAD)
    normed_one = normalize(residual_in, ln1_gain, ln1_bias)
    column_count = qkv_weight.shape[2]
    weight_piece = lax.all_gather(qkv_weight, "dp", axis=0, tiled=True)
    operand = normed_one
    projected = jnp.dot(
        operand, weight_piece.reshape(weight_piece.shape[0], -1), preferred_element_type=jnp.float32
    ).reshape(frame_count, 3, column_count)
    queries = (
        ((projected[:, 0] + qv_bias[0]) * HDIM ** (-0.5))
        .astype(jnp.bfloat16)
        .reshape(frame_count, -1, HDIM)
    )
    key_rows = projected[:, 1].astype(jnp.bfloat16).reshape(frame_count, -1, HDIM)
    value_rows = (projected[:, 2] + qv_bias[1]).astype(jnp.bfloat16).reshape(frame_count, -1, HDIM)
    context = attend(queries, key_rows, value_rows)
    output_rows = lax.all_gather(out_weight, "dp", axis=0, tiled=True)
    carried = residual_in.astype(jnp.float32) + out_bias
    whole_context = gather_directly(context, HEAD, 1)
    split_rows = output_rows.reshape(output_rows.shape[0], head_count, local_width)
    feature_columns = lax.all_to_all(
        split_rows, HEAD, split_axis=1, concat_axis=0, tiled=True
    ).reshape(-1, local_width)
    attended = (
        carried + jnp.dot(whole_context, feature_columns, preferred_element_type=jnp.float32)
    ).astype(jnp.bfloat16)
    normed_two = normalize(attended, ln2_gain, ln2_bias)
    operand = normed_two
    hidden_sums = jnp.dot(
        operand, gather_directly(fc1_weight, "dp", 0), preferred_element_type=jnp.float32
    )
    hidden = jax.nn.gelu(hidden_sums + fc1_bias, approximate=False).astype(jnp.bfloat16)
    down_rows = lax.all_gather(fc2_weight, "dp", axis=0, tiled=True)
    kept = attended.astype(jnp.float32) + fc2_bias
    layer_out = (
        kept
        + own_rows(
            block_term(
                hidden, down_rows, frame_count * lax.axis_size(HEAD), frame_count, local_width
            ),
            HEAD,
        )
    ).astype(jnp.bfloat16)
    return layer_out.reshape(1, 1, group_rows, 4 * local_width)


def solution(mesh):
    torus = Mesh(mesh.devices.reshape(mesh.shape["dp"], 4, 2), ("dp", "head_0", "head_1"))
    return jax.shard_map(
        on_device,
        mesh=torus,
        in_specs=(
            P("dp", HEAD, None, None),
            P(),
            P(),
            P("dp", None, HEAD),
            P(None, HEAD),
            P(HEAD_DP, None),
            P(HEAD),
            P(),
            P(),
            P("dp", HEAD),
            P(HEAD),
            P(HEAD_DP, None),
            P(HEAD),
            P(),
        ),
        out_specs=P("dp", HEAD, None, None),
        check_vma=False,
    )
```

profile of v0, /device:TPU:1, one launch (start us, length us, event | category | flops | bytes accessed | tf_op | source)
XLA Modules:
  0.0 519.1 jit_solution(1292017763583869009)
XLA Ops:
  7.4 2.4 all_to_all.38
  10.3 3.1 reduce.9
  13.4 0.9 reshape.166
  14.3 10.0 %all-to-all-start = ((bf16[32,2,3200]{2,1,0:T(2,128)(2,1)}), bf16[32,2,3200]{2,1,0:T(2,128)(2,1)S(1)}, u32[]{:S(2)}, u32[]{:S(2)}) async-start(bf16[32,2,3200]{2,1,0:T(2,128)(2,1)} %reshape.166), calls=%async_computation | async-start | bytes 819200 | tf_op jit(solution)/shard_map/all_to_all | solution.py:83
  24.7 14.0 %all-to-all-done = bf16[32,2,3200]{2,1,0:T(2,128)(2,1)S(1)} async-done(((bf16[32,2,3200]{2,1,0:T(2,128)(2,1)}), bf16[32,2,3200]{2,1,0:T(2,128)(2,1)S(1)}, u32[]{:S(2)}, u32[]{:S(2)}) %all-to-all-start) | async-done | bytes 409632 | tf_op jit(solution)/shard_map/all_to_all | solution.py:83
  39.0 0.8 gather_fusion
  39.9 0.9 reduce.10
  40.9 17.8 %all_to_all.44 = bf16[32,2,3200]{2,1,0:T(2,128)(2,1)S(1)} all-to-all(bf16[32,2,3200]{2,1,0:T(2,128)(2,1)S(1)} %reshape.168), channel_id=1, replica_groups=mesh['dp'=32,'head_0'=4,'head_1'=2] {'dp'}, dimensions={0} | all-to-all | bytes 819200 | tf_op jit(solution)/shard_map/all_to_all | solution.py:85
  59.1 2.4 reduce
  61.5 0.8 reshape.131
  62.4 1.0 copy.56
  63.4 43.6 %all-gather = bf16[32,4,1280]{2,1,0:T(4,128)(2,1)S(1)} all-gather(bf16[1,4,1280]{2,1,0:T(4,128)(2,1)S(1)} %bitcast.96), channel_id=1, replica_groups=mesh['dp'=32,'head_0'=4,'head_1'=2] {'dp'}, dimensions={0}, use_global_device_ids=true | all-gather | bytes 337920 | tf_op jit(solution)/shard_map/all_gather | solution.py:137
  106.9 0.7 reshape.135
  107.6 1.1 copy.63
  108.7 6.3 %all-to-all-start.3 = ((bf16[128,8,160]{0,2,1:T(8,128)(2,1)}), bf16[128,8,160]{0,2,1:T(8,128)(2,1)S(1)}, u32[]{:S(2)}, u32[]{:S(2)}) async-start(bf16[128,8,160]{0,2,1:T(8,128)(2,1)} %copy.63), calls=%async_computation.3 | async-start | bytes 655360 | tf_op jit(solution)/shard_map/all_to_all | solution.py:141
  115.1 62.0 %all_gather.16 = bf16[1280,3,128]{2,0,1:T(8,128)(2,1)S(1)} all-gather(bf16[40,3,128]{2,0,1:T(8,128)(2,1)S(1)} %copy-done.8), channel_id=1, replica_groups=mesh['dp'=32,'head_0'=4,'head_1'=2] {'dp'}, dimensions={0}, use_global_device_ids=true | all-gather | bytes 1013760 | tf_op jit(solution)/shard_map/all_gather | solution.py:124
  177.9 2.6 convert_reduce_fusion.1
  180.8 0.9 fusion.22
  181.8 1.8 fusion.41
  184.1 1.5 copy.62
  185.9 2.4 fusion.50
  188.4 8.4 %while.10 = (s32[]{:T(128)}, bf16[2,1280,64]{1,2,0:T(8,128)(2,1)}, bf16[2,1280,64]{2,1,0:T(8,128)(2,1)S(1)}, bf16[2,1280,64]{2,1,0:T(8,128)(2,1)S(1)}, bf16[2,1280,64]{2,1,0:T(8,128)(2,1)}, /*index=5*/s32[]{:T(128)}) while((s32[]{:T(128)}, bf16[2,1280,64]{1,2,0:T(8,128)(2,1)}, bf16[2,1280,64]{2,1,0:T(8,128)(2,1)S(1)}, ...), condition=%wide.region_7.8_spmd, body=%wide.region_4.7_spmd.sunk | while | flops 429340160 | bytes 24773784 | solution.py:63
  188.4 1.0 fusion.97
  189.4 1.0 fusion.98
  190.6 1.3 fusion.99
  191.9 0.7 copy-done.6
  192.6 1.0 fusion.97
  193.6 1.0 fusion.98
  194.8 1.3 fusion.99
  196.1 0.7 copy-done.6
  196.8 2.6 broadcast_in_dim.36
  199.5 10.7 %all-to-all-start.2 = ((bf16[8,1280,128]{1,2,0:T(8,128)(2,1)}), bf16[8,1280,128]{1,2,0:T(8,128)(2,1)S(1)}, u32[]{:S(2)}, u32[]{:S(2)}) async-start(bf16[8,1280,128]{1,2,0:T(8,128)(2,1)} %broadcast_in_dim.36), calls=%async_computation.2 | async-start | bytes 5242880 | tf_op jit(solution)/shard_map/all_to_all | solution.py:23
  210.8 0.9 copy.64
  211.7 62.7 %all-to-all-done.2 = bf16[8,1280,128]{1,2,0:T(8,128)(2,1)S(1)} async-done(((bf16[8,1280,128]{1,2,0:T(8,128)(2,1)}), bf16[8,1280,128]{1,2,0:T(8,128)(2,1)S(1)}, u32[]{:S(2)}, u32[]{:S(2)}) %all-to-all-start.2) | async-done | bytes 2621472 | tf_op jit(solution)/shard_map/all_to_all | solution.py:23
  274.4 2.3 fusion.46
  276.7 1.4 broadcast_in_dim.37
  278.1 4.8 all-to-all-start.4
  283.0 31.5 %all-gather.10.cloned.1.call-done = bf16[32,20,1280]{2,1,0:T(8,128)(2,1)} async-done(((bf16[1,20,1280]{2,1,0:T(8,128)(2,1)}), bf16[32,20,1280]{2,1,0:T(8,128)(2,1)}) %all-gather.10.cloned.1.call-update) | async-done | bytes 1638416 | tf_op jit(solution)/shard_map/all_gather | solution.py:153
  314.4 3.8 reshape.150
  318.3 94.6 %all-gather.8.cloned.1.call-done = bf16[1280,1280]{0,1:T(8,128)(2,1)} async-done(((bf16[1280,160]{0,1:T(8,128)(2,1)}), bf16[1280,1280]{0,1:T(8,128)(2,1)}) %all-gather.8.cloned.1.call-update) | async-done | bytes 3276816 | tf_op jit(solution)/shard_map/all_gather | solution.py:47
  412.9 2.6 convert_reduce_fusion
  415.8 0.9 fusion.18
  416.8 15.6 %convolution_convert_fusion = bf16[1280,1280]{0,1:T(8,128)(2,1)} fusion(bf16[640,1280]{1,0:T(8,128)(2,1)} %reshape.150, bf16[1280,640]{1,0:T(8,128)(2,1)} %bitcast.24, bf16[1280,1280]{0,1:T(8,128)(2,1)S(1)} %copy-done.1, f32[1280]{0:T(1024)S(1)} %copy-done.15, f32[1280]{0:T(1024)S(1)} %copy-done.16, f32[1280]{0:T(1024)S(1)} %add_rsqrt_fusion, ...), kind=kOutput, calls=%fused_computation.25 | convolution fusion | flops 4259840000 | bytes 9853440 | tf_op jit(solution)/shard_map/dot_general | solution.py:91
  432.4 4.0 copy.71
  436.5 38.1 %reduce-scatter.3.cloned.1.call-done = bf16[2560,160]{0,1:T(8,128)(2,1)} async-done(((bf16[10240,160]{0,1:T(8,128)(2,1)}), bf16[2560,160]{0,1:T(8,128)(2,1)}) %reduce-scatter.3.cloned.1.call-update) | async-done | bytes 819216 | tf_op jit(solution)/shard_map/reduce_scatter | solution.py:33
  474.6 33.6 %reduce-scatter.5.cloned.1.call-done = bf16[1280,160]{0,1:T(8,128)(2,1)} async-done(((bf16[2560,160]{0,1:T(8,128)(2,1)}), bf16[1280,160]{0,1:T(8,128)(2,1)}) %reduce-scatter.5.cloned.1.call-update) | async-done | bytes 409616 | tf_op jit(solution)/shard_map/reduce_scatter | solution.py:33
  508.2 1.2 add_convert_fusion.1
  509.7 1.6 reshape.138
  (80 shorter events, 5.6 us)
Async XLA Ops:
  7.4 17.0 %copy-start.18 = (s32[32]{0:T(128)S(1)}, s32[32]{0:T(128)}, u32[]{:S(2)}) copy-start(s32[32]{0:T(128)} %param.29) | copy-start | bytes 388
  14.3 24.4 %all-to-all-start = ((bf16[32,2,3200]{2,1,0:T(2,128)(2,1)}), bf16[32,2,3200]{2,1,0:T(2,128)(2,1)S(1)}, u32[]{:S(2)}, u32[]{:S(2)}) async-start(bf16[32,2,3200]{2,1,0:T(2,128)(2,1)} %reshape.166), calls=%async_computation | async-start | bytes 819200 | tf_op jit(solution)/shard_map/all_to_all | solution.py:83
  24.3 153.6 %all-gather.6.cloned.1.call-start = ((), (), s32[]{:S(2)}) async-start(), calls=%async_computation.7 | async-start | bytes 3686400 | tf_op jit(solution)/shard_map/all_gather | solution.py:47
  40.8 22.6 %copy-start.9 = (bf16[4,1280]{1,0:T(4,128)(2,1)S(1)}, bf16[4,1280]{1,0:T(4,128)(2,1)}, u32[]{:S(2)}) copy-start(bf16[4,1280]{1,0:T(4,128)(2,1)} %param.21) | copy-start | bytes 30724
  59.1 56.0 %copy-start.8 = (bf16[40,3,128]{2,0,1:T(8,128)(2,1)S(1)}, bf16[40,3,128]{2,0,1:T(8,128)(2,1)}, u32[]{:S(2)}) copy-start(bf16[40,3,128]{2,0,1:T(8,128)(2,1)} %param.19) | copy-start | bytes 92164
  63.4 114.4 %copy-start.10 = (f32[2,128]{1,0:T(2,128)S(1)}, f32[2,128]{1,0:T(2,128)}, u32[]{:S(2)}) copy-start(f32[2,128]{1,0:T(2,128)} %param.20) | copy-start | bytes 3076
  108.7 88.1 %all-to-all-start.3 = ((bf16[128,8,160]{0,2,1:T(8,128)(2,1)}), bf16[128,8,160]{0,2,1:T(8,128)(2,1)S(1)}, u32[]{:S(2)}, u32[]{:S(2)}) async-start(bf16[128,8,160]{0,2,1:T(8,128)(2,1)} %copy.63), calls=%async_computation.3 | async-start | bytes 655360 | tf_op jit(solution)/shard_map/all_to_all | solution.py:141
  177.9 3.9 copy-start.13
  177.9 3.9 copy-start.14
  177.9 2.9 copy-start
  189.4 1.1 copy-start.4
  189.4 1.2 copy-start.5
  191.9 0.7 copy-start.6
  193.6 1.1 copy-start.4
  193.6 1.2 copy-start.5
  196.1 0.7 copy-start.6
  199.5 74.9 %copy-start.2 = (bf16[1280,160]{0,1:T(8,128)(2,1)S(1)}, bf16[1280,160]{0,1:T(8,128)(2,1)}, u32[]{:S(2)}) copy-start(bf16[1280,160]{0,1:T(8,128)(2,1)} %copy.56) | copy-start | bytes 1228804
  199.5 74.9 %copy-start.12 = (f32[160]{0:T(256)S(1)}, f32[160]{0:T(256)}, u32[]{:S(2)}) copy-start(f32[160]{0:T(256)} %param.22) | copy-start | bytes 1924
  199.5 74.9 %all-to-all-start.2 = ((bf16[8,1280,128]{1,2,0:T(8,128)(2,1)}), bf16[8,1280,128]{1,2,0:T(8,128)(2,1)S(1)}, u32[]{:S(2)}, u32[]{:S(2)}) async-start(bf16[8,1280,128]{1,2,0:T(8,128)(2,1)} %broadcast_in_dim.36), calls=%async_computation.2 | async-start | bytes 5242880 | tf_op jit(solution)/shard_map/all_to_all | solution.py:23
  210.2 66.5 %copy-start.7 = (bf16[40,640]{1,0:T(8,128)(2,1)S(1)}, bf16[40,640]{1,0:T(8,128)(2,1)}, u32[]{:S(2)}) copy-start(bf16[40,640]{1,0:T(8,128)(2,1)} %param.25) | copy-start | bytes 153604
  210.2 104.2 %all-gather.10.cloned.1.call-start = ((), (), s32[]{:S(2)}) async-start(), calls=%async_computation.11 | async-start | bytes 2027520 | tf_op jit(solution)/shard_map/all_gather | solution.py:153
  210.8 202.1 %all-gather.8.cloned.1.call-start = ((), (), s32[]{:S(2)}) async-start(), calls=%async_computation.8 | async-start | bytes 3686400 | tf_op jit(solution)/shard_map/all_gather | solution.py:47
  278.1 138.6 %all-to-all-start.4 = ((bf16[32,40,640]{2,1,0:T(8,128)(2,1)}), bf16[32,40,640]{2,1,0:T(8,128)(2,1)}, u32[]{:S(2)}, u32[]{:S(2)}) async-start(bf16[32,40,640]{2,1,0:T(8,128)(2,1)} %broadcast_in_dim.37), calls=%async_computation.4 | async-start | bytes 3276800 | tf_op jit(solution)/shard_map/all_to_all | solution.py:23
  282.9 191.7 %reduce-scatter.3.cloned.1.call-start = ((), (), s32[]{:S(2)}) async-start(), calls=%async_computation.9 | async-start | bytes 4096000 | tf_op jit(solution)/shard_map/reduce_scatter | solution.py:33
  318.2 98.5 %copy-start.15 = (f32[1280]{0:T(1024)S(1)}, f32[1280]{0:T(1024)}, u32[]{:S(2)}) copy-start(f32[1280]{0:T(1024)} %param.24) | copy-start | bytes 15364
  318.3 98.5 %copy-start.16 = (f32[1280]{0:T(1024)S(1)}, f32[1280]{0:T(1024)}, u32[]{:S(2)}) copy-start(f32[1280]{0:T(1024)} %param.23) | copy-start | bytes 15364
  318.3 98.5 %copy-start.17 = (f32[640]{0:T(1024)S(1)}, f32[640]{0:T(1024)}, u32[]{:S(2)}) copy-start(f32[640]{0:T(1024)} %param.26) | copy-start | bytes 7684
  412.9 2.9 copy-start.1
  436.4 71.8 %copy-start.3 = (bf16[1280,160]{0,1:T(8,128)(2,1)S(1)}, bf16[1280,160]{0,1:T(8,128)(2,1)}, u32[]{:S(2)}) copy-start(bf16[1280,160]{0,1:T(8,128)(2,1)} %fusion.46) | copy-start | bytes 1228804
  436.4 71.8 %copy-start.11 = (f32[160]{0:T(256)S(1)}, f32[160]{0:T(256)}, u32[]{:S(2)}) copy-start(f32[160]{0:T(256)} %param.28) | copy-start | bytes 1924
  436.4 71.8 %reduce-scatter.5.cloned.1.call-start = ((), (), s32[]{:S(2)}) async-start(), calls=%async_computation.10 | async-start | bytes 1228800 | tf_op jit(solution)/shard_map/reduce_scatter | solution.py:33
Sparse Core Ops, SparseCore 0:
  63.5 93.1 all-gather.5
  436.6 37.9 reduce-scatter.2
Sparse Core Ops, SparseCore 1:
  212.5 101.8 all-gather.9
  316.9 95.9 all-gather.7
  474.7 33.5 reduce-scatter.4
where the time goes:
time: 528 us; the launch traced here: 519 us
  waiting for transfers between devices  275 us (52%)
  blocking collectives  123 us (23%)
  starting transfers between devices  32.1 us (6%)
  local copies, waits for them, and re-layouts  29.2 us (6%)
  matrix products  24.4 us (5%)
  other arithmetic  19.4 us (4%)
  between operations  15.6 us (3%)
    all_gather x2, waiting for transfers between devices, normalize(): whole_rows = lax.all_gather(residual_in, HEAD, axis=1, tiled=True)  94.6 us
    reduce_scatter x2, waiting for transfers between devices, own_rows(): total = lax.psum_scatter(total, axis, scatter_dimension=0, tiled=True)  71.7 us
    all_to_all x2, waiting for transfers between devices, sent_to_all(): return lax.all_to_all(copies, axis, split_axis=0, concat_axis=0, tiled=True)  62.7 us
    all_gather x1, blocking collectives, on_device(): weight_piece = lax.all_gather(qkv_weight, 'dp', axis=0, tiled=True)  62 us
    all_gather x1, blocking collectives, on_device(): output_rows = lax.all_gather(out_weight, 'dp', axis=0, tiled=True)  43.6 us
    all_gather x1, waiting for transfers between devices, on_device(): down_rows = lax.all_gather(fc2_weight, 'dp', axis=0, tiled=True)  31.5 us
    all_to_all x1, blocking collectives, regroup(): lax.all_to_all(picked, 'dp', split_axis=0, concat_axis=0, tiled=True)  17.8 us
    dot_general x1, matrix products, block_term(): product = jnp.dot(operand, weight_rows, preferred_element_type=jnp.float32)  15.6 us
  transfers between devices with their start and end apart: 9, of which 6 were waited for; matrix products, arithmetic and copies ran while one was open for 6% of the time, Pallas kernels for 0%

commit v1 on v0

v1 whole, which is shorter than its diff:
```python
import functools

import jax
import jax.numpy as jnp
from jax import lax
from jax.experimental import pallas as pl
from jax.experimental.pallas import tpu as pltpu
from jax.sharding import Mesh
from jax.sharding import PartitionSpec as P

MESH = pl.DeviceIdType.MESH
BF16 = jnp.bfloat16
F32 = jnp.float32
EPS = 1e-05
HDIM = 64
DP = ("x", "zl", "c")
HEAD = ("y", "zh")
HEAD_DP = ("y", "zh", "x", "zl", "c")

D = 1280
HALF = 160
TILES = 112
PIECE = 7


def remote(src, dst, send, recv, device):
    return pltpu.make_async_remote_copy(
        src_ref=src, dst_ref=dst, send_sem=send, recv_sem=recv,
        device_id=device, device_id_type=MESH,
    )


class Ring4:
    def __init__(self, slab, half, i, device, send, recv, first=None):
        up, down = lax.rem(i + 1, 4), lax.rem(i + 3, 4)
        own = slab(i)
        self.one = [
            remote(own, own, send.at[0], recv.at[0], device(up)),
            remote(own, own, send.at[1], recv.at[1], device(down)),
        ]
        self.two = [
            remote(half(down, 0), half(down, 0), send.at[2], recv.at[2], device(up)),
            remote(half(up, 1), half(up, 1), send.at[3], recv.at[3], device(down)),
        ]

    def start(self):
        for copy in self.one:
            copy.start()

    def forward(self):
        for copy, nxt in zip(self.one, self.two):
            copy.wait_recv()
            nxt.start()

    def arrive(self):
        for copy in self.two:
            copy.wait_recv()

    def drain(self):
        for copy in self.one + self.two:
            copy.wait_send()


class Ring8:
    def __init__(self, slab, i, device, send, recv):
        up, down = lax.rem(i + 1, 8), lax.rem(i + 7, 8)
        self.steps = []
        for s in range(4):
            older = slab(lax.rem(i + 8 - s, 8))
            copies = [remote(older, older, send.at[2 * s], recv.at[2 * s], device(up))]
            if s < 3:
                newer = slab(lax.rem(i + s, 8))
                copies.append(
                    remote(newer, newer, send.at[2 * s + 1], recv.at[2 * s + 1], device(down))
                )
            self.steps.append(copies)

    def start(self, s):
        for copy in self.steps[s]:
            copy.start()

    def arrive(self, s):
        for copy in self.steps[s]:
            copy.wait_recv()

    def drain(self):
        for copies in self.steps:
            for copy in copies:
                copy.wait_send()


def layer_norm(floats, gain, shift):
    center = jnp.sum(floats, axis=-1, keepdims=True) * (1.0 / D)
    moved = floats - center
    spread = jnp.sum(moved * moved, axis=-1, keepdims=True) * (1.0 / D)
    return (moved * lax.rsqrt(spread + EPS) * gain + shift).astype(BF16)


def dot(a, b):
    return jnp.dot(a, b, preferred_element_type=F32)


def kernel(
    order, fin, qkv_in, fc1_in, tail_in, bias_in, norms,
    out,
    p1, p2, xg, wq, w1, w2, wo, pair, bg, xr, xn, qs, kv, cx, att, n2, pk, ra, rb, rc, rd, fo,
    local, s_p1, r_p1, s_p2, r_p2, s_pair, r_pair, s_bias, r_bias,
    s_zq, r_zq, s_zo, r_zo, s_z1, r_z1, s_z2, r_z2,
    s_xq, r_xq, s_xo, r_xo, s_x1, r_x1, s_x2, r_x2,
    s_yx, r_yx, s_yo, r_yo, s_yn, r_yn, s_d, r_d, s_cx, r_cx, s_rs, r_rs, s_out, r_out,
):
    x, zl, c = lax.axis_index("x"), lax.axis_index("zl"), lax.axis_index("c")
    y, zh = lax.axis_index("y"), lax.axis_index("zh")
    z = zh * 4 + zl
    clip = x * 8 + zl * 2 + c

    def at(x_=x, zl_=zl, c_=c, y_=y, zh_=zh):
        return (x_, zl_, c_, y_, zh_)

    def at_z(z_):
        return at(zl_=lax.rem(z_, 4), zh_=z_ // 4)

    sibling = at(c_=1 - c)

    barrier = pltpu.get_barrier_semaphore()

    def greet(device):
        pl.semaphore_signal(barrier, inc=1, device_id=device, device_id_type=MESH)

    @pl.loop(1, 32)
    def _(i):
        t = lax.rem(clip + i, 32)
        greet(at(x_=t // 8, zl_=lax.rem(t // 2, 4), c_=lax.rem(t, 2)))

    @pl.loop(0, 16)
    def _(i):
        t = lax.rem(x * 4 + zl + i, 16)
        greet(at(x_=t // 4, zl_=lax.rem(t, 4), zh_=1 - zh))

    greet(at(c_=1 - c, zh_=1 - zh))
    for i in range(1, 4):
        greet(at(y_=lax.rem(y + i, 4)))
        greet(at(y_=lax.rem(y + i, 4), zh_=1 - zh))
    pl.semaphore_wait(barrier, 54)

    to_pair = remote(tail_in.at[1 - c], pair.at[c], s_pair, r_pair, sibling)
    to_pair.start()
    own_pair = pltpu.make_async_copy(tail_in.at[c], pair.at[c], local.at[0])

    def piece_of(x_, zl_, c_):
        return c_ * 16 + x_ * 4 + zl_

    @pl.loop(1, 32)
    def _(i):
        t = lax.rem(clip + i, 32)
        x_, zl_, c_ = t // 8, lax.rem(t // 2, 4), lax.rem(t, 2)
        remote(fin.at[piece_of(x_, zl_, c_)], p1.at[clip], s_p1, r_p1, at(x_=x_, zl_=zl_, c_=c_)).start()

    keep_one = pltpu.make_async_copy(fin.at[piece_of(x, zl, c)], p1.at[clip], r_p1)
    keep_one.start()

    own_q = pltpu.make_async_copy(qkv_in, wq.at[zh, x, zl, c], local.at[1])
    own_1 = pltpu.make_async_copy(fc1_in, w1.at[zh, x, zl, c], local.at[2])
    own_b = pltpu.make_async_copy(bias_in, bg.at[y * 2 + zh], local.at[3])
    for copy in (own_q, own_1, own_b):
        copy.start()

    bias_sends = []
    for i in range(4):
        for other in range(2):
            if i or other:
                device = at(y_=lax.rem(y + i, 4), zh_=(1 - zh) if other else zh)
                n = i * 2 + other
                bias_sends.append(
                    remote(bias_in, bg.at[y * 2 + zh], s_bias.at[n], r_bias.at[n], device)
                )

    zq = Ring8(lambda i: wq.at[i // 4, x, lax.rem(i, 4), c], z, at_z, s_zq, r_zq)
    zo = Ring8(lambda i: wo.at[c, y, i // 4, x, lax.rem(i, 4)], z, at_z, s_zo, r_zo)
    z1 = Ring8(lambda i: w1.at[i // 4, x, lax.rem(i, 4), c], z, at_z, s_z1, r_z1)
    z2 = Ring8(lambda i: w2.at[c, i // 4, x, lax.rem(i, 4)], z, at_z, s_z2, r_z2)

    def at_x(i):
        return at(x_=i)

    def at_y(i):
        return at(y_=i)

    xq = Ring4(lambda i: wq.at[:, i, :, c], lambda i, h: wq.at[h, i, :, c], x, at_x, s_xq, r_xq)
    xo = Ring4(lambda i: wo.at[c, y, :, i], lambda i, h: wo.at[c, y, h, i], x, at_x, s_xo, r_xo)
    x1 = Ring4(lambda i: w1.at[:, i, :, c], lambda i, h: w1.at[h, i, :, c], x, at_x, s_x1, r_x1)
    x2 = Ring4(lambda i: w2.at[c, :, i], lambda i, h: w2.at[c, h, i], x, at_x, s_x2, r_x2)
    yx = Ring4(
        lambda i: xg.at[i, :, pl.ds(0, 100)],
        lambda i, h: xg.at[i, h, pl.ds(0, 100)],
        y, at_y, s_yx, r_yx,
    )
    yo = Ring4(lambda i: wo.at[c, i], lambda i, h: wo.at[c, i, h], y, at_y, s_yo, r_yo)
    yn = Ring4(
        lambda i: n2.at[i], lambda i, h: n2.at[i, pl.ds(80 * h, 80)], y, at_y, s_yn, r_yn
    )
    dq = remote(wq.at[:, :, :, c], wq.at[:, :, :, c], s_d.at[0], r_d.at[0], sibling)
    do = remote(wo.at[c], wo.at[c], s_d.at[1], r_d.at[1], sibling)
    d1 = remote(w1.at[:, :, :, c], w1.at[:, :, :, c], s_d.at[2], r_d.at[2], sibling)
    d2 = remote(w2.at[c], w2.at[c], s_d.at[3], r_d.at[3], sibling)
    dkv = remote(kv.at[c], kv.at[c], s_d.at[4], r_d.at[4], sibling)

    own_q.wait()
    zq.start(0)
    for copy in bias_sends:
        copy.start()
    own_pair.start()
    own_pair.wait()
    to_pair.wait_recv()
    wo[c, y, zh, x, zl, 0:4] = pair[0, 0:4]
    wo[c, y, zh, x, zl, 4:8] = pair[1, 0:4]
    w2[c, zh, x, zl, 0:20] = pair[0, 4:24]
    w2[c, zh, x, zl, 20:40] = pair[1, 4:24]
    zo.start(0)
    for s in range(4):
        zq.arrive(s)
        zo.arrive(s)
        if s < 3:
            zq.start(s + 1)
            zo.start(s + 1)
    own_1.wait()
    own_b.wait()

    pltpu.make_async_copy(p1, p1, r_p1).wait()

    @pl.loop(0, 32)
    def _(s):
        p2[s] = p1[order[s]]

    slot = x * 8 + zl * 2 + zh
    place = xg.at[y, zh, pl.ds(PIECE * (x * 4 + zl), PIECE)]

    @pl.loop(1, 32)
    def _(i):
        t = lax.rem(slot + i, 32)
        remote(
            p2.at[t], place, s_p2, r_p2, at(x_=t // 8, zl_=lax.rem(t // 2, 4), zh_=lax.rem(t, 2))
        ).start()

    keep_two = pltpu.make_async_copy(p2.at[slot], place, r_p2)
    keep_two.start()

    xq.start()
    xo.start()
    z1.start(0)
    z2.start(0)
    xq.forward()
    xo.forward()
    pltpu.make_async_copy(xg.at[y], xg.at[y], r_p2).wait()
    yx.start()
    for s in range(4):
        z1.arrive(s)
        z2.arrive(s)
        if s < 3:
            z1.start(s + 1)
            z2.start(s + 1)
        if s == 0:
            xq.arrive()
            dq.start()
        if s == 1:
            yx.forward()
    x1.start()
    x2.start()
    for copy in bias_sends:
        copy.wait_recv()
    yx.arrive()

    @pl.loop(0, 10)
    def _(t):
        rows = []
        for b in range(8):
            parts = [
                xg[b // 2, b % 2, pl.ds(lt * 20 + t * 2, 2)].reshape(16, 128) for lt in range(5)
            ]
            rows.append(jnp.concatenate(parts, axis=1))
        for j in range(4):
            whole = jnp.concatenate([r[:, 160 * j : 160 * j + 160] for r in rows], axis=1)
            start = pl.multiple_of(t * 16, 16)
            xr[j, pl.ds(start, 16)] = whole
            xn[j, pl.ds(start, 16)] = layer_norm(whole.astype(F32), norms[0:1], norms[1:2])

    dq.wait_recv()

    @pl.loop(0, 4)
    def _(j):
        left = xn[j]
        rows = pl.ds(pl.multiple_of(j * HALF, HALF), HALF)
        for h in range(2):
            prod = dot(left, wq[h].reshape(D, 384))
            biases = bg[y * 2 + h]
            lanes = slice(128 * h, 128 * h + 128)
            qs[rows, lanes] = ((prod[:, 0:128] + biases[3:4, 0:128]) * HDIM ** (-0.5)).astype(BF16)
            kv[c, 0, rows, lanes] = prod[:, 128:256].astype(BF16)
            kv[c, 1, rows, lanes] = (prod[:, 256:384] + biases[4:5, 0:128]).astype(BF16)

    dkv.start()
    xo.arrive()
    yo.start()
    dkv.wait_recv()

    head_of = lax.broadcasted_iota(jnp.int32, (HALF, 256), 1) // HDIM

    def attend(j):
        rows = pl.ds(pl.multiple_of(j * HALF, HALF), HALF)
        q = qs[rows, :]
        zero = jnp.zeros_like(q)
        stacked = jnp.concatenate([jnp.where(head_of == h, q, zero) for h in range(4)], axis=0)
        keys = kv[:, 0].reshape(D, 256)
        scores = lax.dot_general(
            stacked, keys, (((1,), (1,)), ((), ())), preferred_element_type=F32
        )
        weights = jnp.exp(scores - jnp.max(scores, axis=-1, keepdims=True))
        total = jnp.sum(weights, axis=-1, keepdims=True)
        mixed = dot(weights.astype(BF16), kv[:, 1].reshape(D, 256)) / total
        context = jnp.zeros((HALF, 256), F32)
        for h in range(4):
            context = context + jnp.where(head_of == h, mixed[h * HALF : (h + 1) * HALF], 0.0)
        return context.astype(BF16)

    @pl.loop(1, 4)
    def _(i):
        j = lax.rem(y + i, 4)
        cx[4 + j] = attend(j)
        remote(cx.at[4 + j], cx.at[y], s_cx.at[i - 1], r_cx.at[i - 1], at(y_=j)).start()

    yo.forward()
    cx[y] = attend(y)
    x1.forward()
    x2.forward()
    yo.arrive()
    do.start()
    for i in range(1, 4):
        remote(cx.at[0], cx.at[0], s_cx.at[i - 1], r_cx.at[i - 1], sibling).wait_recv()
    do.wait_recv()

    def whole_bias(row):
        return jnp.concatenate([bg[h, row : row + 1, 0:160] for h in range(8)], axis=1)

    context = jnp.concatenate([cx[i] for i in range(4)], axis=1)
    product = jnp.concatenate(
        [dot(context, wo[h].reshape(1024, 640)) for h in range(2)], axis=1
    )
    attended = (xr[y].astype(F32) + whole_bias(1) + product).astype(BF16)
    att[...] = attended.astype(F32) + whole_bias(2)
    n2[y] = layer_norm(attended.astype(F32), norms[2:3], norms[3:4])
    yn.start()
    x1.arrive()
    x2.arrive()
    d1.start()
    d2.start()
    yn.forward()
    d1.wait_recv()
    d2.wait_recv()
    yn.arrive()

    for j in range(4):
        left = n2[j]
        parts = []
        for h in range(2):
            sums = dot(left, w1[h].reshape(D, 640)) + bg[y * 2 + h, 0:1, :]
            parts.append((0.5 * sums * (1.0 + lax.erf(sums * 0.5**0.5))).astype(BF16))
        hidden = jnp.concatenate(parts, axis=1)
        share = jnp.concatenate(
            [dot(hidden, w2[h].reshape(D, 640)) for h in range(2)], axis=1
        )
        share = share + jnp.where(y == j, att[...], 0.0)
        for b in range(8):
            pk[b // 2, b % 2, :, 160 * j : 160 * j + 160] = share[:, 160 * b : 160 * b + 160].astype(
                BF16
            )

    up, down, far = lax.rem(y + 1, 4), lax.rem(y + 3, 4), lax.rem(y + 2, 4)
    sums = [
        remote(pk.at[far, 0], ra, s_rs.at[0], r_rs.at[0], at(y_=up)),
        remote(pk.at[far, 1], rb, s_rs.at[1], r_rs.at[1], at(y_=down)),
        remote(pk.at[up], rc, s_rs.at[2], r_rs.at[2], at(y_=up)),
        remote(pk.at[down], rd, s_rs.at[3], r_rs.at[3], at(y_=down)),
    ]
    sums[0].start()
    sums[1].start()
    sums[0].wait_recv()
    pk[up, 0] = (pk[up, 0].astype(F32) + ra[...].astype(F32)).astype(BF16)
    sums[2].start()
    sums[1].wait_recv()
    pk[down, 1] = (pk[down, 1].astype(F32) + rb[...].astype(F32)).astype(BF16)
    sums[3].start()
    sums[2].wait_recv()
    sums[3].wait_recv()
    fo[...] = (pk[y].astype(F32) + rc[...].astype(F32) + rd[...].astype(F32)).astype(BF16)

    mine = pl.ds(pl.multiple_of(c * HALF, HALF), HALF)
    across = remote(fo.at[1 - zh], out.at[mine], s_out.at[0], r_out, at(c_=zh, zh_=1 - zh))
    across.start()
    keep_out = pltpu.make_async_copy(fo.at[zh], out.at[mine], r_out)
    beside = remote(fo.at[zh], out.at[mine], s_out.at[1], r_out, sibling)

    @pl.when(c == zh)
    def _():
        keep_out.start()

    @pl.when(c != zh)
    def _():
        beside.start()

    pltpu.make_async_copy(out, out, r_out).wait()

    across.wait_send()

    @pl.when(c != zh)
    def _():
        beside.wait_send()

    to_pair.wait_send()
    pltpu.make_async_copy(p1.at[pl.ds(0, 31)], p1.at[pl.ds(0, 31)], s_p1).wait()
    pltpu.make_async_copy(p1.at[pl.ds(0, 31)], p1.at[pl.ds(0, 31)], s_p2).wait()
    for copy in bias_sends + sums + [dq, do, d1, d2, dkv]:
        copy.wait_send()
    for i in range(1, 4):
        remote(cx.at[0], cx.at[0], s_cx.at[i - 1], r_cx.at[i - 1], sibling).wait_send()
    for ring in (zq, zo, z1, z2, xq, xo, x1, x2, yx, yo, yn):
        ring.drain()


def slot_order(server_list):
    clip_count = server_list.shape[0]
    indices = jnp.arange(clip_count, dtype=jnp.int32)
    earlier = (server_list[None, :] < server_list[:, None]) | (
        server_list[None, :] == server_list[:, None]
    ) & (indices[None, :] < indices[:, None])
    slot_of = jnp.sum(earlier.astype(jnp.int32), axis=1)
    return jnp.sum(jnp.where(slot_of[None, :] == indices[:, None], indices[None, :], 0), axis=1)


def on_device(
    frames_in, ln1_gain, ln1_bias, qkv_weight, qv_bias, out_weight, out_bias,
    ln2_gain, ln2_bias, fc1_weight, fc1_bias, fc2_weight, fc2_bias, server_of_clip,
):
    clip_order = slot_order(server_of_clip)
    tiles = frames_in[0, 0].reshape(2, 20, 8, 5, 128).transpose(0, 3, 1, 2, 4)
    fin = jnp.pad(tiles.reshape(2, 100, 8, 128), ((0, 0), (0, TILES - 100), (0, 0), (0, 0)))
    fin = fin.reshape(32, PIECE, 8, 128)
    tail = jnp.concatenate([out_weight, fc2_weight], axis=0).reshape(24, 2, 640).transpose(1, 0, 2)

    def row(v):
        return jnp.pad(v, (0, 640 - v.shape[0]))[None]

    biases = jnp.concatenate(
        [row(fc1_bias), row(out_bias), row(fc2_bias), row(qv_bias[0]), row(qv_bias[1]),
         jnp.zeros((3, 640), F32)], axis=0,
    )
    norms = jnp.stack([ln1_gain, ln1_bias, ln2_gain, ln2_bias])
    vmem = pl.BlockSpec(memory_space=pltpu.VMEM)
    smem = pl.BlockSpec(memory_space=pltpu.SMEM)
    dma = pltpu.SemaphoreType.DMA
    V = pltpu.VMEM
    out = pl.pallas_call(
        kernel,
        out_shape=jax.ShapeDtypeStruct((320, 640), BF16),
        in_specs=[smem] + [vmem] * 6,
        out_specs=vmem,
        scratch_shapes=[
            V((32, PIECE, 8, 128), BF16),
            V((32, PIECE, 8, 128), BF16),
            V((4, 2, TILES, 8, 128), BF16),
            V((2, 4, 4, 2, 40, 384), BF16),
            V((2, 4, 4, 2, 40, 640), BF16),
            V((2, 2, 4, 4, 40, 640), BF16),
            V((2, 4, 2, 4, 4, 8, 640), BF16),
            V((2, 24, 640), BF16),
            V((8, 8, 640), F32),
            V((4, HALF, D), BF16),
            V((4, HALF, D), BF16),
            V((640, 256), BF16),
            V((2, 2, 640, 256), BF16),
            V((8, HALF, 256), BF16),
            V((HALF, D), F32),
            V((4, HALF, D), BF16),
            V((4, 2, HALF, 640), BF16),
            V((HALF, 640), BF16),
            V((HALF, 640), BF16),
            V((2, HALF, 640), BF16),
            V((2, HALF, 640), BF16),
            V((2, HALF, 640), BF16),
            dma((4,)),
            dma, dma, dma, dma, dma, dma, dma((8,)), dma((8,)),
            dma((7,)), dma((7,)), dma((7,)), dma((7,)), dma((7,)), dma((7,)), dma((7,)), dma((7,)),
            dma((4,)), dma((4,)), dma((4,)), dma((4,)), dma((4,)), dma((4,)), dma((4,)), dma((4,)),
            dma((4,)), dma((4,)), dma((4,)), dma((4,)), dma((4,)), dma((4,)),
            dma((5,)), dma((5,)), dma((3,)), dma((3,)), dma((4,)), dma((4,)), dma((2,)), dma,
        ],
        compiler_params=pltpu.CompilerParams(
            collective_id=0, has_side_effects=True, vmem_limit_bytes=60 * 2**20
        ),
    )(clip_order, fin, qkv_weight.reshape(40, 384), fc1_weight, tail, biases, norms)
    return out.reshape(1, 1, 320, 640)


def solution(mesh):
    torus = Mesh(mesh.devices.reshape(4, 4, 2, 4, 2), ("x", "zl", "c", "y", "zh"))
    return jax.shard_map(
        on_device,
        mesh=torus,
        in_specs=(
            P(DP, HEAD, None, None), P(), P(), P(DP, None, HEAD), P(None, HEAD), P(HEAD_DP, None),
            P(HEAD), P(), P(), P(DP, HEAD), P(HEAD), P(HEAD_DP, None), P(HEAD), P(),
        ),
        out_specs=P(DP, HEAD, None, None),
        check_vma=False,
    )
```

time: 528 us -> 154 us (0.29); the launches traced: 519 us -> 154 us
  waiting for transfers between devices: 275 us -> 0 us
  Pallas kernels: 0 us -> 141 us
  blocking collectives: 123 us -> 0 us
  starting transfers between devices: 32.1 us -> 0 us
  matrix products: 24.4 us -> 0 us
  local copies, waits for them, and re-layouts: 29.2 us -> 10.2 us
  other arithmetic: 19.4 us -> 2.33 us
  between operations: 15.6 us -> 0.07 us
    pallas_call x0 -> x1, Pallas kernels: none -> 141 us  [on_device(): pl.pallas_call(kernel, out_shape=jax.ShapeDtypeStruct((320, 640), BF16),...]
    all_gather x3 -> x0, waiting for transfers between devices: 126 us -> none  [the longest x2 94.6 us: normalize(): whole_rows = lax.all_gather(residual_in, HEAD, axis=1, tiled=True)]
    all_gather x2 -> x0, blocking collectives: 106 us -> none  [the longest x1 62 us: on_device(): weight_piece = lax.all_gather(qkv_weight, 'dp', axis=0, tiled=True)]
    all_to_all x4 -> x0, waiting for transfers between devices: 76.7 us -> none  [the longest x2 62.7 us: sent_to_all(): return lax.all_to_all(copies, axis, split_axis=0, concat_axis=0, tiled=True)]
    reduce_scatter x2 -> x0, waiting for transfers between devices: 71.7 us -> none  [own_rows(): total = lax.psum_scatter(total, axis, scatter_dimension=0, tiled=True)]
    all_to_all x4 -> x0, starting transfers between devices: 31.9 us -> none  [the longest x2 15.5 us: sent_to_all(): return lax.all_to_all(copies, axis, split_axis=0, concat_axis=0, tiled=True)]
    dot_general x7 -> x0, matrix products: 24.4 us -> none  [the longest x1 15.6 us: block_term(): product = jnp.dot(operand, weight_rows, preferred_element_type=jnp.float32)]
    all_to_all x1 -> x0, blocking collectives: 17.8 us -> none  [regroup(): lax.all_to_all(picked, 'dp', split_axis=0, concat_axis=0, tiled=True)]
  transfers between devices with their start and end apart: 9 -> 0, of which waited for: 6 -> 0; matrix products, arithmetic and copies ran while one was open for 6% -> 0% of each run, Pallas kernels for 0% -> 0%
where the time goes in v1:
time: 154 us
  Pallas kernels  141 us (92%)
  local copies, waits for them, and re-layouts  10.2 us (7%)
  other arithmetic  2.33 us (2%)
    pallas_call x1, Pallas kernels, on_device(): pl.pallas_call(kernel, out_shape=jax.ShapeDtypeStruct((320, 640), BF16),...  141 us

profile of v1, /device:TPU:1, one launch (start us, length us, event | category | flops | bytes accessed | tf_op | source)
XLA Modules:
  0.0 153.9 jit_solution(15845196797662068352)
XLA Ops:
  0.0 0.0 copy-start
  0.0 0.0 copy-start.3
  0.0 0.0 copy-start.2
  0.0 0.0 copy-start.1
  0.0 0.6 copy-done.3
  0.7 0.2 convert_reduce_fusion
  0.8 0.7 select_reduce_fusion.order
  1.5 0.8 slice_bitcast_fusion
  2.3 0.0 copy-done.2
  2.3 0.7 pad.19
  3.0 0.7 pad.20
  3.7 0.7 stack.15
  4.4 0.7 stack.16
  5.1 0.7 stack.17
  5.8 0.7 stack.18
  6.5 0.6 pad_maximum_fusion.1.norms
  7.1 0.6 concatenate.7.bias_in
  7.8 0.0 copy-done
  7.8 0.6 copy_bitcast_fusion.qkv_in
  8.4 0.9 pad_maximum_fusion
  9.2 0.6 copy.27
  9.9 0.0 copy-done.1
  9.9 0.1 copy.20
  10.0 0.8 pad.18
  10.8 141.3 %shard_map.136 = bf16[320,640]{1,0:T(8,128)(2,1)} custom-call(s32[32]{0:T(128)} %select_reduce_fusion.order, bf16[32,7,8,128]{3,2,1,0:T(8,128)(2,1)} %bitcast.22, bf16[40,384]{1,0:T(8,128)(2,1)} %copy_bitcast_fusion.qkv_in, bf16[40,640]{1,0:T(8,128)(2,1)} %fc1_in.1, bf16[2,24,640]{2,1,0:T(8,128)(2,1)} %bitcast.27, f32[8,640]{1,0:T(8,128)} %concatenate.7.bias_in, ...), custom_call_target="tpu_custom_call" | custom-call | tf_op jit(solution)/shard_map/pallas_call | solution.py:461
  152.1 1.8 %copy.29 = bf16[1,1,320,640]{3,2,1,0:T(8,128)(2,1)} copy(bf16[1,1,320,640]{3,2,1,0:T(8,128)(2,1)} %bitcast.23) | data formatting | bytes 819200
  (8 shorter events, 0.0 us)
Async XLA Ops:
  0.0 7.8 %copy-start = (bf16[40,3,128]{2,0,1:T(8,128)(2,1)S(1)}, bf16[40,3,128]{2,0,1:T(8,128)(2,1)}, u32[]{:S(2)}) copy-start(bf16[40,3,128]{2,0,1:T(8,128)(2,1)} %param.17) | copy-start | bytes 92164
  0.0 0.7 copy-start.3
  0.0 2.3 %copy-start.2 = (f32[640]{0:T(1024)S(1)}, f32[640]{0:T(1024)}, u32[]{:S(2)}) copy-start(f32[640]{0:T(1024)} %param.24) | copy-start | bytes 7684
  0.0 9.9 %copy-start.1 = (bf16[1,1,320,640]{3,2,1,0:T(8,128)(2,1)S(1)}, bf16[1,1,320,640]{3,2,1,0:T(8,128)(2,1)}, u32[]{:S(2)}) copy-start(bf16[1,1,320,640]{3,2,1,0:T(8,128)(2,1)} %param.14) | copy-start | bytes 1228804

commit v2 on v1

v2 whole, which is shorter than its diff:
```python
import functools

import jax
import jax.numpy as jnp
from jax import lax
from jax.experimental import pallas as pl
from jax.experimental.pallas import tpu as pltpu
from jax.sharding import Mesh
from jax.sharding import PartitionSpec as P

MESH = pl.DeviceIdType.MESH
BF16 = jnp.bfloat16
F32 = jnp.float32
EPS = 1e-05
HDIM = 64
DP = ("x", "zl", "c")
HEAD = ("y", "zh")
HEAD_DP = ("y", "zh", "x", "zl", "c")

D = 1280
HALF = 160
TILES = 112
PIECE = 7
CHUNKS = 5
ROWS = 32


def remote(src, dst, send, recv, device):
    return pltpu.make_async_remote_copy(
        src_ref=src, dst_ref=dst, send_sem=send, recv_sem=recv,
        device_id=device, device_id_type=MESH,
    )


class Ring4:
    def __init__(self, slab, half, i, device, send, recv, base=0):
        up, down = lax.rem(i + 1, 4), lax.rem(i + 3, 4)
        own = slab(i)

        def sems(n):
            return send.at[base + n], recv.at[base + n]

        self.one = [
            remote(own, own, *sems(0), device(up)),
            remote(own, own, *sems(1), device(down)),
        ]
        self.two = [
            remote(half(down, 0), half(down, 0), *sems(2), device(up)),
            remote(half(up, 1), half(up, 1), *sems(3), device(down)),
        ]

    def start(self):
        for copy in self.one:
            copy.start()

    def forward(self):
        for copy, nxt in zip(self.one, self.two):
            copy.wait_recv()
            nxt.start()

    def arrive(self):
        for copy in self.two:
            copy.wait_recv()

    def drain(self):
        for copy in self.one + self.two:
            copy.wait_send()


class Ring8:
    def __init__(self, slab, i, device, send, recv):
        up, down = lax.rem(i + 1, 8), lax.rem(i + 7, 8)
        self.steps = []
        for s in range(4):
            older = slab(lax.rem(i + 8 - s, 8))
            copies = [remote(older, older, send.at[2 * s], recv.at[2 * s], device(up))]
            if s < 3:
                newer = slab(lax.rem(i + s, 8))
                copies.append(
                    remote(newer, newer, send.at[2 * s + 1], recv.at[2 * s + 1], device(down))
                )
            self.steps.append(copies)

    def start(self, s):
        for copy in self.steps[s]:
            copy.start()

    def arrive(self, s):
        for copy in self.steps[s]:
            copy.wait_recv()

    def relay(self, s):
        self.arrive(s)
        if s < 3:
            self.start(s + 1)

    def drain(self):
        for copies in self.steps:
            for copy in copies:
                copy.wait_send()


def layer_norm(floats, gain, shift):
    center = jnp.sum(floats, axis=-1, keepdims=True) * (1.0 / D)
    moved = floats - center
    spread = jnp.sum(moved * moved, axis=-1, keepdims=True) * (1.0 / D)
    return (moved * lax.rsqrt(spread + EPS) * gain + shift).astype(BF16)


def dot(a, b):
    return jnp.dot(a, b, preferred_element_type=F32)


def kernel(
    order, frames, qkv_in, fc1_in, out_in, fc2_in, b_qv, b_out, b_fc1, b_fc2, g1, s1, g2, s2,
    out,
    fin, p1, p2, xg, wq, w1, w2, wo, tail, pair, bias, bg, xr, xn, qs, kv, cx, att, n2, pk,
    ra, rb, rc, rd, fo,
    local, s_p1, r_p1, s_p2, r_p2, s_pair, r_pair, s_bias, r_bias,
    s_zq, r_zq, s_zo, r_zo, s_z1, r_z1, s_z2, r_z2,
    s_xq, r_xq, s_xo, r_xo, s_x1, r_x1, s_x2, r_x2,
    s_yx, r_yx, s_yo, r_yo, s_yn, r_yn, s_d, r_d, s_cx, r_cx, s_rs, r_rs, s_out, s_next, r_out,
):
    x, zl, c = lax.axis_index("x"), lax.axis_index("zl"), lax.axis_index("c")
    y, zh = lax.axis_index("y"), lax.axis_index("zh")
    z = zh * 4 + zl
    clip = x * 8 + zl * 2 + c

    def at(x_=x, zl_=zl, c_=c, y_=y, zh_=zh):
        return (x_, zl_, c_, y_, zh_)

    def at_z(z_):
        return at(zl_=lax.rem(z_, 4), zh_=z_ // 4)

    def at_x(i):
        return at(x_=i)

    def at_y(i):
        return at(y_=i)

    sibling = at(c_=1 - c)

    barrier = pltpu.get_barrier_semaphore()

    def greet(device):
        pl.semaphore_signal(barrier, inc=1, device_id=device, device_id_type=MESH)

    @pl.loop(0, 16)
    def _(i):
        t = lax.rem(x * 4 + zl + i, 16)
        greet(at(x_=t // 4, zl_=lax.rem(t, 4), zh_=1 - zh))

    @pl.loop(1, 32)
    def _(i):
        t = lax.rem(clip + i, 32)
        greet(at(x_=t // 8, zl_=lax.rem(t // 2, 4), c_=lax.rem(t, 2)))

    greet(at(c_=1 - c, zh_=1 - zh))
    for i in range(1, 4):
        greet(at(y_=lax.rem(y + i, 4)))
        greet(at(y_=lax.rem(y + i, 4), zh_=1 - zh))

    for half in range(2):
        for tile in range(100):
            rt, lt = half * 20 + tile // 5, tile % 5
            k = half * TILES + tile
            fin[k // PIECE, k % PIECE] = frames[8 * rt : 8 * rt + 8, 128 * lt : 128 * lt + 128]
        for tile in range(100, TILES):
            k = half * TILES + tile
            fin[k // PIECE, k % PIECE] = jnp.zeros((8, 128), BF16)
    for h in range(2):
        tail[h, 0:4] = out_in[:, 640 * h : 640 * h + 640]
        tail[h, 4:24] = fc2_in[:, 640 * h : 640 * h + 640]
    for t in range(3):
        wq[zh, x, zl, c, :, 128 * t : 128 * t + 128] = qkv_in[:, t, :]
    bias[0:1, :] = b_fc1[...]
    bias[1:2, 0:160] = b_out[...]
    bias[2:3, 0:160] = b_fc2[...]
    bias[3:5, 0:128] = b_qv[...]
    own_1 = pltpu.make_async_copy(fc1_in, w1.at[zh, x, zl, c], local.at[0])
    own_1.start()

    zq = Ring8(lambda i: wq.at[i // 4, x, lax.rem(i, 4), c], z, at_z, s_zq, r_zq)
    zo = Ring8(lambda i: wo.at[c, y, i // 4, x, lax.rem(i, 4)], z, at_z, s_zo, r_zo)
    z1 = Ring8(lambda i: w1.at[i // 4, x, lax.rem(i, 4), c], z, at_z, s_z1, r_z1)
    z2 = Ring8(lambda i: w2.at[c, i // 4, :, lax.rem(i, 4)], z, at_z, s_z2, r_z2)
    xq = Ring4(lambda i: wq.at[:, i, :, c], lambda i, h: wq.at[h, i, :, c], x, at_x, s_xq, r_xq)
    xo = Ring4(lambda i: wo.at[c, y, :, i], lambda i, h: wo.at[c, y, h, i], x, at_x, s_xo, r_xo)
    x1 = Ring4(lambda i: w1.at[:, i, :, c], lambda i, h: w1.at[h, i, :, c], x, at_x, s_x1, r_x1)
    x2 = Ring4(
        lambda i: w2.at[c, zh, i, zl],
        lambda i, h: w2.at[c, zh, i, zl, pl.ds(24 * h, 24 - 8 * h)],
        x, at_x, s_x2, r_x2,
    )
    yo = Ring4(lambda i: wo.at[c, i], lambda i, h: wo.at[c, i, h], y, at_y, s_yo, r_yo)

    def yx(t):
        tiles = pl.ds(t * 20, 20)
        return Ring4(
            lambda i: xg.at[i, :, tiles], lambda i, h: xg.at[i, h, tiles], y, at_y, s_yx, r_yx, t * 4
        )

    def yn(t):
        def rows(first, count):
            return pl.ds(pl.multiple_of(t * ROWS + first, 16), count)

        return Ring4(
            lambda i: n2.at[i, rows(0, ROWS)], lambda i, h: n2.at[i, rows(16 * h, 16)],
            y, at_y, s_yn, r_yn, t * 4,
        )

    dq = remote(wq.at[:, :, :, c], wq.at[:, :, :, c], s_d.at[0], r_d.at[0], sibling)
    d1 = remote(w1.at[:, :, :, c], w1.at[:, :, :, c], s_d.at[1], r_d.at[1], sibling)
    d2 = remote(w2.at[c], w2.at[c], s_d.at[2], r_d.at[2], sibling)
    dkv = remote(kv.at[c], kv.at[c], s_d.at[3], r_d.at[3], sibling)
    do = []
    for n in range(4):
        part = wo.at[c, lax.rem(y + (0, 1, 3, 2)[n], 4)]
        do.append(remote(part, part, s_d.at[4 + n], r_d.at[4 + n], sibling))
    bias_sends = []
    for i in range(4):
        for other in range(2):
            if i or other:
                device = at(y_=lax.rem(y + i, 4), zh_=(1 - zh) if other else zh)
                n = i * 2 + other
                bias_sends.append(
                    remote(bias, bg.at[y * 2 + zh], s_bias.at[n], r_bias.at[n], device)
                )
    own_b = pltpu.make_async_copy(bias, bg.at[y * 2 + zh], local.at[1])
    own_pair = pltpu.make_async_copy(tail.at[c], pair.at[c], local.at[2])
    to_pair = remote(tail.at[1 - c], pair.at[c], s_pair, r_pair, sibling)

    pl.semaphore_wait(barrier, 54)

    to_pair.start()
    zq.start(0)
    own_b.start()
    own_pair.start()

    def piece_of(x_, zl_, c_):
        return c_ * 16 + x_ * 4 + zl_

    def regroup_sends(first, last):
        @pl.loop(first, last)
        def _(i):
            t = lax.rem(clip + i, 32)
            x_, zl_, c_ = t // 8, lax.rem(t // 2, 4), lax.rem(t, 2)
            remote(
                fin.at[piece_of(x_, zl_, c_)], p1.at[clip], s_p1, r_p1, at(x_=x_, zl_=zl_, c_=c_)
            ).start()

    keep_one = pltpu.make_async_copy(fin.at[piece_of(x, zl, c)], p1.at[clip], r_p1)
    keep_one.start()
    regroup_sends(1, 9)
    own_pair.wait()
    to_pair.wait_recv()
    wo[c, y, zh, x, zl, 0:4] = pair[0, 0:4]
    wo[c, y, zh, x, zl, 4:8] = pair[1, 0:4]
    w2[c, zh, x, zl, 0:20] = pair[0, 4:24]
    w2[c, zh, x, zl, 20:40] = pair[1, 4:24]
    zo.start(0)
    zq.relay(0)
    regroup_sends(9, 17)
    zo.relay(0)
    zq.relay(1)
    regroup_sends(17, 25)
    zo.relay(1)
    zq.relay(2)
    regroup_sends(25, 32)
    zo.relay(2)
    x2.start()
    for copy in bias_sends:
        copy.start()
    zq.arrive(3)
    xq.start()
    own_1.wait()
    own_b.wait()

    pltpu.make_async_copy(p1, p1, r_p1).wait()

    @pl.loop(0, 32)
    def _(s):
        p2[s] = p1[order[s]]

    slot = x * 8 + zl * 2 + zh
    place = xg.at[y, zh, pl.ds(PIECE * (x * 4 + zl), PIECE)]

    @pl.loop(1, 32)
    def _(i):
        t = lax.rem(slot + i, 32)
        remote(
            p2.at[t], place, s_p2, r_p2, at(x_=t // 8, zl_=lax.rem(t // 2, 4), zh_=lax.rem(t, 2))
        ).start()

    keep_two = pltpu.make_async_copy(p2.at[slot], place, r_p2)
    keep_two.start()

    z1.start(0)
    x2.forward()
    zo.arrive(3)
    xo.start()
    xq.forward()
    xo.forward()
    x2.arrive()
    z2.start(0)
    xq.arrive()
    dq.start()
    pltpu.make_async_copy(xg.at[y], xg.at[y], r_p2).wait()

    yx(0).start()
    yx(1).start()
    z1.relay(0)
    for copy in bias_sends:
        copy.wait_recv()
    yx(0).forward()
    yx(2).start()
    dq.wait_recv()

    def project(t):
        @pl.loop(0, 2)
        def _(u):
            first = t * 20 + u * 10
            blocks = []
            for b in range(8):
                parts = [
                    jnp.concatenate(
                        [xg[b // 2, b % 2, first + lt], xg[b // 2, b % 2, first + 5 + lt]], axis=0
                    )
                    for lt in range(5)
                ]
                blocks.append(jnp.concatenate(parts, axis=1))
            start = pl.multiple_of(t * ROWS + u * 16, 16)
            inner = pl.multiple_of(u * 16, 16)
            for j in range(4):
                whole = jnp.concatenate(
                    [block[:, 160 * j : 160 * j + 160] for block in blocks], axis=1
                )
                xr[j, pl.ds(start, 16)] = whole
                xn[j, pl.ds(inner, 16)] = layer_norm(whole.astype(F32), g1[...], s1[...])

        left = xn[...].reshape(4 * ROWS, D)
        for h in range(2):
            prod = dot(left, wq[h].reshape(D, 384))
            biases = bg[y * 2 + h]
            lanes = slice(128 * h, 128 * h + 128)
            query = ((prod[:, 0:128] + biases[3:4, 0:128]) * HDIM ** (-0.5)).astype(BF16)
            key = prod[:, 128:256].astype(BF16)
            value = (prod[:, 256:384] + biases[4:5, 0:128]).astype(BF16)
            for j in range(4):
                rows = pl.ds(pl.multiple_of(j * HALF + t * ROWS, 16), ROWS)
                part = slice(ROWS * j, ROWS * j + ROWS)
                qs[rows, lanes] = query[part]
                kv[c, 0, rows, lanes] = key[part]
                kv[c, 1, rows, lanes] = value[part]

    @pl.loop(0, CHUNKS)
    def _(t):
        @pl.when(t < CHUNKS - 1)
        def _():
            yx(t + 1).forward()

        @pl.when(t < CHUNKS - 3)
        def _():
            yx(t + 3).start()

        for n in range(3):
            @pl.when(t == n)
            def _():
                z1.relay(n + 1)

        @pl.when(t == 2)
        def _():
            z2.relay(0)

        yx(t).arrive()
        project(t)

    dkv.start()
    x1.start()
    xo.arrive()
    yo.start()
    do[0].start()
    z2.relay(1)
    dkv.wait_recv()

    head_of = lax.broadcasted_iota(jnp.int32, (HALF, 256), 1) // HDIM

    def attend(j):
        rows = pl.ds(pl.multiple_of(j * HALF, HALF), HALF)
        q = qs[rows, :]
        zero = jnp.zeros_like(q)
        stacked = jnp.concatenate([jnp.where(head_of == h, q, zero) for h in range(4)], axis=0)
        keys = kv[:, 0].reshape(D, 256)
        scores = lax.dot_general(
            stacked, keys, (((1,), (1,)), ((), ())), preferred_element_type=F32
        )
        weights = jnp.exp(scores - jnp.max(scores, axis=-1, keepdims=True))
        total = jnp.sum(weights, axis=-1, keepdims=True)
        mixed = dot(weights.astype(BF16), kv[:, 1].reshape(D, 256)) / total
        context = jnp.zeros((HALF, 256), F32)
        for h in range(4):
            context = context + jnp.where(head_of == h, mixed[h * HALF : (h + 1) * HALF], 0.0)
        return context.astype(BF16)

    @pl.loop(1, 4)
    def _(i):
        j = lax.rem(y + i, 4)
        cx[4 + j] = attend(j)
        remote(cx.at[4 + j], cx.at[y], s_cx.at[i - 1], r_cx.at[i - 1], at(y_=j)).start()

        @pl.when(i == 1)
        def _():
            z2.relay(2)

        @pl.when(i == 2)
        def _():
            yo.forward()
            do[1].start()
            do[2].start()

    x1.forward()
    z2.arrive(3)
    d2.start()
    cx[y] = attend(y)
    yo.arrive()
    do[3].start()
    x1.arrive()
    d1.start()
    for i in range(1, 4):
        remote(cx.at[0], cx.at[0], s_cx.at[i - 1], r_cx.at[i - 1], sibling).wait_recv()
    for copy in do:
        copy.wait_recv()

    def whole_bias(row):
        return jnp.concatenate([bg[h, row : row + 1, 0:160] for h in range(8)], axis=1)

    context = jnp.concatenate([cx[i] for i in range(4)], axis=1)
    product = jnp.concatenate(
        [dot(context, wo[h].reshape(1024, 640)) for h in range(2)], axis=1
    )
    attended = (xr[y].astype(F32) + whole_bias(1) + product).astype(BF16)
    att[...] = attended.astype(F32) + whole_bias(2)
    n2[y] = layer_norm(attended.astype(F32), g2[...], s2[...])
    yn(0).start()
    yn(1).start()
    yn(0).forward()
    yn(2).start()
    d1.wait_recv()
    d2.wait_recv()

    up, down, far = lax.rem(y + 1, 4), lax.rem(y + 3, 4), lax.rem(y + 2, 4)

    def rows_of(t):
        return pl.ds(pl.multiple_of(t * ROWS, ROWS), ROWS)

    def sums(t):
        r, n = rows_of(t), 4 * t
        return [
            remote(pk.at[far, 0, r], ra.at[r], s_rs.at[n], r_rs.at[n], at(y_=up)),
            remote(pk.at[far, 1, r], rb.at[r], s_rs.at[n + 1], r_rs.at[n + 1], at(y_=down)),
            remote(pk.at[up, :, r], rc.at[:, r], s_rs.at[n + 2], r_rs.at[n + 2], at(y_=up)),
            remote(pk.at[down, :, r], rd.at[:, r], s_rs.at[n + 3], r_rs.at[n + 3], at(y_=down)),
        ]

    def feed_forward(t):
        r = rows_of(t)
        left = jnp.concatenate([n2[j, r] for j in range(4)], axis=0)
        parts = []
        for h in range(2):
            total = dot(left, w1[h].reshape(D, 640)) + bg[y * 2 + h, 0:1, :]
            parts.append((0.5 * total * (1.0 + lax.erf(total * 0.5**0.5))).astype(BF16))
        hidden = jnp.concatenate(parts, axis=1)
        share = jnp.concatenate(
            [dot(hidden, w2[h].reshape(D, 640)) for h in range(2)], axis=1
        )
        kept = att[r]
        for j in range(4):
            part = share[ROWS * j : ROWS * j + ROWS] + jnp.where(y == j, kept, 0.0)
            for b in range(8):
                pk[b // 2, b % 2, r, 160 * j : 160 * j + 160] = part[
                    :, 160 * b : 160 * b + 160
                ].astype(BF16)
        sums(t)[0].start()
        sums(t)[1].start()

    def add_and_pass(t):
        r = rows_of(t)
        copies = sums(t)
        copies[0].wait_recv()
        pk[up, 0, r] = (pk[up, 0, r].astype(F32) + ra[r].astype(F32)).astype(BF16)
        copies[2].start()
        copies[1].wait_recv()
        pk[down, 1, r] = (pk[down, 1, r].astype(F32) + rb[r].astype(F32)).astype(BF16)
        copies[3].start()

    def out_rows(t):
        return out.at[pl.ds(pl.multiple_of(c * HALF + t * ROWS, ROWS), ROWS)]

    def finish(t):
        r = rows_of(t)
        copies = sums(t)
        copies[2].wait_recv()
        copies[3].wait_recv()
        fo[:, r] = (pk[y, :, r].astype(F32) + rc[:, r].astype(F32) + rd[:, r].astype(F32)).astype(
            BF16
        )
        remote(fo.at[1 - zh, r], out_rows(t), s_out, r_out, at(c_=zh, zh_=1 - zh)).start()

        @pl.when(c == zh)
        def _():
            pltpu.make_async_copy(fo.at[zh, r], out_rows(t), r_out).start()

        @pl.when(c != zh)
        def _():
            remote(fo.at[zh, r], out_rows(t), s_next, r_out, sibling).start()

    @pl.loop(0, CHUNKS)
    def _(t):
        @pl.when(t < CHUNKS - 1)
        def _():
            yn(t + 1).forward()

        @pl.when(t < CHUNKS - 3)
        def _():
            yn(t + 3).start()

        yn(t).arrive()
        feed_forward(t)

        @pl.when(t > 0)
        def _():
            add_and_pass(t - 1)

        @pl.when(t > 1)
        def _():
            finish(t - 2)

    add_and_pass(CHUNKS - 1)
    finish(CHUNKS - 2)
    finish(CHUNKS - 1)

    pltpu.make_async_copy(out, out, r_out).wait()

    pltpu.make_async_copy(fo.at[0], fo.at[0], s_out).wait()

    @pl.when(c != zh)
    def _():
        pltpu.make_async_copy(fo.at[0], fo.at[0], s_next).wait()

    to_pair.wait_send()
    pltpu.make_async_copy(p1.at[pl.ds(0, 31)], p1.at[pl.ds(0, 31)], s_p1).wait()
    pltpu.make_async_copy(p1.at[pl.ds(0, 31)], p1.at[pl.ds(0, 31)], s_p2).wait()
    for copy in bias_sends + do + [dq, d1, d2, dkv]:
        copy.wait_send()
    for i in range(1, 4):
        remote(cx.at[0], cx.at[0], s_cx.at[i - 1], r_cx.at[i - 1], sibling).wait_send()
    for ring in (zq, zo, z1, z2, xq, xo, x1, x2, yo):
        ring.drain()

    @pl.loop(0, CHUNKS)
    def _(t):
        yx(t).drain()
        yn(t).drain()
        for copy in sums(t):
            copy.wait_send()


def slot_order(server_list):
    clip_count = server_list.shape[0]
    indices = jnp.arange(clip_count, dtype=jnp.int32)
    earlier = (server_list[None, :] < server_list[:, None]) | (
        server_list[None, :] == server_list[:, None]
    ) & (indices[None, :] < indices[:, None])
    slot_of = jnp.sum(earlier.astype(jnp.int32), axis=1)
    return jnp.sum(jnp.where(slot_of[None, :] == indices[:, None], indices[None, :], 0), axis=1)


def on_device(
    frames_in, ln1_gain, ln1_bias, qkv_weight, qv_bias, out_weight, out_bias,
    ln2_gain, ln2_bias, fc1_weight, fc1_bias, fc2_weight, fc2_bias, server_of_clip,
):
    clip_order = slot_order(server_of_clip)
    vmem = pl.BlockSpec(memory_space=pltpu.VMEM)
    smem = pl.BlockSpec(memory_space=pltpu.SMEM)
    dma = pltpu.SemaphoreType.DMA
    V = pltpu.VMEM
    out = pl.pallas_call(
        kernel,
        out_shape=jax.ShapeDtypeStruct((320, 640), BF16),
        in_specs=[smem] + [vmem] * 13,
        out_specs=vmem,
        scratch_shapes=[
            V((32, PIECE, 8, 128), BF16),
            V((32, PIECE, 8, 128), BF16),
            V((32, PIECE, 8, 128), BF16),
            V((4, 2, TILES, 8, 128), BF16),
            V((2, 4, 4, 2, 40, 384), BF16),
            V((2, 4, 4, 2, 40, 640), BF16),
            V((2, 2, 4, 4, 40, 640), BF16),
            V((2, 4, 2, 4, 4, 8, 640), BF16),
            V((2, 24, 640), BF16),
            V((2, 24, 640), BF16),
            V((8, 640), F32),
            V((8, 8, 640), F32),
            V((4, HALF, D), BF16),
            V((4, ROWS, D), BF16),
            V((640, 256), BF16),
            V((2, 2, 640, 256), BF16),
            V((8, HALF, 256), BF16),
            V((HALF, D), F32),
            V((4, HALF, D), BF16),
            V((4, 2, HALF, 640), BF16),
            V((HALF, 640), BF16),
            V((HALF, 640), BF16),
            V((2, HALF, 640), BF16),
            V((2, HALF, 640), BF16),
            V((2, HALF, 640), BF16),
            dma((3,)),
            dma, dma, dma, dma, dma, dma, dma((8,)), dma((8,)),
            dma((7,)), dma((7,)), dma((7,)), dma((7,)), dma((7,)), dma((7,)), dma((7,)), dma((7,)),
            dma((4,)), dma((4,)), dma((4,)), dma((4,)), dma((4,)), dma((4,)), dma((4,)), dma((4,)),
            dma((4 * CHUNKS,)), dma((4 * CHUNKS,)), dma((4,)), dma((4,)),
            dma((4 * CHUNKS,)), dma((4 * CHUNKS,)),
            dma((8,)), dma((8,)), dma((3,)), dma((3,)), dma((4 * CHUNKS,)), dma((4 * CHUNKS,)),
            dma, dma, dma,
        ],
        compiler_params=pltpu.CompilerParams(
            collective_id=0, has_side_effects=True, vmem_limit_bytes=60 * 2**20
        ),
    )(
        clip_order, frames_in.reshape(320, 640), qkv_weight, fc1_weight, out_weight, fc2_weight,
        qv_bias, out_bias[None], fc1_bias[None], fc2_bias[None],
        ln1_gain[None], ln1_bias[None], ln2_gain[None], ln2_bias[None],
    )
    return out.reshape(1, 1, 320, 640)


def solution(mesh):
    torus = Mesh(mesh.devices.reshape(4, 4, 2, 4, 2), ("x", "zl", "c", "y", "zh"))
    return jax.shard_map(
        on_device,
        mesh=torus,
        in_specs=(
            P(DP, HEAD, None, None), P(), P(), P(DP, None, HEAD), P(None, HEAD), P(HEAD_DP, None),
            P(HEAD), P(), P(), P(DP, HEAD), P(HEAD), P(HEAD_DP, None), P(HEAD), P(),
        ),
        out_specs=P(DP, HEAD, None, None),
        check_vma=False,
    )
```

time: 154 us -> 130 us (0.84)
  Pallas kernels: 141 us -> 123 us
  local copies, waits for them, and re-layouts: 10.2 us -> 5.42 us
    pallas_call x1, Pallas kernels: 141 us -> 123 us  [on_device(): pl.pallas_call(kernel, out_shape=jax.ShapeDtypeStruct((320, 640), BF16),...]
    broadcast_in_dim x6 -> x5, local copies, waits for them, and re-layouts: 0.02 us -> 2.98 us  [the longest x1 0.6 us: on_device(): ln1_gain[None]]
    another operation x4 -> x0, local copies, waits for them, and re-layouts: 2.8 us -> none  [on_device(): norms = jnp.stack([ln1_gain, ln1_bias, ln2_gain, ln2_bias])]
    pad x5 -> x0, local copies, waits for them, and re-layouts: 2.18 us -> none  [the longest x4 1.37 us: row(): return jnp.pad(v, (0, 640 - v.shape[0]))[None]]
where the time goes in v2:
time: 130 us
  Pallas kernels  123 us (95%)
  local copies, waits for them, and re-layouts  5.42 us (4%)
  other arithmetic  1.57 us (1%)
    pallas_call x1, Pallas kernels, on_device(): pl.pallas_call(kernel, out_shape=jax.ShapeDtypeStruct((320, 640), BF16),...  123 us

profile of v2, /device:TPU:1, one launch (start us, length us, event | category | flops | bytes accessed | tf_op | source)
XLA Modules:
  0.0 129.7 jit_solution(13711255633191992643)
XLA Ops:
  0.0 0.0 copy-start.5
  0.0 0.0 copy-start.1
  0.0 0.0 copy-start.2
  0.0 0.0 copy-start.3
  0.0 0.0 copy-start.4
  0.0 0.9 convert_reduce_fusion
  0.9 0.0 copy-start
  1.0 0.7 select_reduce_fusion.order
  1.6 0.0 copy-done.5
  1.6 0.6 broadcast_in_dim.42.b_fc1
  2.2 0.0 copy-done.1
  2.2 0.6 broadcast_in_dim.44.g1
  2.8 0.0 copy-done.2
  2.8 0.6 broadcast_in_dim.45.s1
  3.4 0.0 copy-done.3
  3.4 0.6 broadcast_in_dim.46.g2
  4.0 0.0 copy-done.4
  4.0 0.6 broadcast_in_dim.47.s2
  4.6 0.0 copy-done
  4.6 0.6 copy.16.qkv_in
  5.2 122.6 %shard_map.136 = bf16[320,640]{1,0:T(8,128)(2,1)} custom-call(s32[32]{0:T(128)} %select_reduce_fusion.order, bf16[320,640]{1,0:T(8,128)(2,1)} %bitcast.5, bf16[40,3,128]{2,1,0:T(4,128)(2,1)} %copy.16.qkv_in, bf16[40,640]{1,0:T(8,128)(2,1)} %fc1_in.1, bf16[4,1280]{1,0:T(4,128)(2,1)} %out_in.1, bf16[20,1280]{1,0:T(8,128)(2,1)} %fc2_in.1, f32[2,128]{1,0:T(2,128)} %b_qv.1, ...), custom_call_target="tpu_custom_call" | custom-call | tf_op jit(solution)/shard_map/pallas_call | solution.py:587
  127.9 1.8 %copy.18 = bf16[1,1,320,640]{3,2,1,0:T(8,128)(2,1)} copy(bf16[1,1,320,640]{3,2,1,0:T(8,128)(2,1)} %bitcast.4) | data formatting | bytes 819200
Async XLA Ops:
  0.0 1.6 %copy-start.5 = (f32[640]{0:T(1024)S(1)}, f32[640]{0:T(1024)}, u32[]{:S(2)}) copy-start(f32[640]{0:T(1024)} %param.24) | copy-start | bytes 7684
  0.0 2.2 %copy-start.1 = (f32[1280]{0:T(1024)S(1)}, f32[1280]{0:T(1024)}, u32[]{:S(2)}) copy-start(f32[1280]{0:T(1024)} %param.15) | copy-start | bytes 15364
  0.0 2.8 %copy-start.2 = (f32[1280]{0:T(1024)S(1)}, f32[1280]{0:T(1024)}, u32[]{:S(2)}) copy-start(f32[1280]{0:T(1024)} %param.16) | copy-start | bytes 15364
  0.0 3.4 %copy-start.3 = (f32[1280]{0:T(1024)S(1)}, f32[1280]{0:T(1024)}, u32[]{:S(2)}) copy-start(f32[1280]{0:T(1024)} %param.21) | copy-start | bytes 15364
  0.0 4.0 %copy-start.4 = (f32[1280]{0:T(1024)S(1)}, f32[1280]{0:T(1024)}, u32[]{:S(2)}) copy-start(f32[1280]{0:T(1024)} %param.22) | copy-start | bytes 15364
  0.9 3.7 %copy-start = (bf16[40,3,128]{2,0,1:T(8,128)(2,1)S(1)}, bf16[40,3,128]{2,0,1:T(8,128)(2,1)}, u32[]{:S(2)}) copy-start(bf16[40,3,128]{2,0,1:T(8,128)(2,1)} %param.17) | copy-start | bytes 92164

commit v3 on v2

--- a/solution.py
+++ b/solution.py
@@ -19,8 +19,8 @@
 
 D = 1280
 HALF = 160
-TILES = 112
-PIECE = 7
+TILES = 100
+PIECE = 6
 CHUNKS = 5
 ROWS = 32
 
@@ -112,14 +112,16 @@
 
 
 def kernel(
-    order, frames, qkv_in, fc1_in, out_in, fc2_in, b_qv, b_out, b_fc1, b_fc2, g1, s1, g2, s2,
+    servers, frames_hbm, qkv_hbm, fc1_in, out_hbm, fc2_hbm, qv_hbm, bo_hbm, b1_hbm, b2_hbm,
+    g1_hbm, s1_hbm, g2_hbm, s2_hbm,
     out,
-    fin, p1, p2, xg, wq, w1, w2, wo, tail, pair, bias, bg, xr, xn, qs, kv, cx, att, n2, pk,
+    keys, slots, order, frames, qkv_in, out_in, fc2_in, b_qv, b_out, b_fc1, b_fc2, g1, s1, g2, s2,
+    norms, fin, p1, p2, xg, wq, w1, w2, wo, tail, pair, bias, bg, xr, xn, qs, kv, cs, cx, att, n2, pk,
     ra, rb, rc, rd, fo,
-    local, s_p1, r_p1, s_p2, r_p2, s_pair, r_pair, s_bias, r_bias,
+    fetch, local, s_p1, r_p1, s_p2, r_p2, s_more, r_more, s_last, s_pair, r_pair, s_bias, r_bias,
     s_zq, r_zq, s_zo, r_zo, s_z1, r_z1, s_z2, r_z2,
     s_xq, r_xq, s_xo, r_xo, s_x1, r_x1, s_x2, r_x2,
-    s_yx, r_yx, s_yo, r_yo, s_yn, r_yn, s_d, r_d, s_cx, r_cx, s_rs, r_rs, s_out, s_next, r_out,
+    s_yx, r_yx, s_yo, r_yo, s_yn, r_yn, s_d, r_d, s_kv, r_kv, s_cx, r_cx, s_rs, r_rs, s_out, s_next, r_out,
 ):
     x, zl, c = lax.axis_index("x"), lax.axis_index("zl"), lax.axis_index("c")
     y, zh = lax.axis_index("y"), lax.axis_index("zh")
@@ -140,6 +142,16 @@
 
     sibling = at(c_=1 - c)
 
+    fetches = [
+        pltpu.make_async_copy(src, dst, fetch.at[n])
+        for n, (src, dst) in enumerate(
+            [(frames_hbm, frames), (out_hbm, out_in), (fc2_hbm, fc2_in), (qkv_hbm, qkv_in),
+             (qv_hbm, b_qv), (bo_hbm, b_out), (b1_hbm, b_fc1), (b2_hbm, b_fc2), (g1_hbm, g1),
+             (s1_hbm, s1), (g2_hbm, g2), (s2_hbm, s2), (fc1_in, w1.at[zh, x, zl, c])]
+        )
+    ]
+    for copy in fetches:
+        copy.start()
     barrier = pltpu.get_barrier_semaphore()
 
     def greet(device):
@@ -160,25 +172,27 @@
         greet(at(y_=lax.rem(y + i, 4)))
         greet(at(y_=lax.rem(y + i, 4), zh_=1 - zh))
 
+    for copy in fetches:
+        copy.wait()
+
     for half in range(2):
         for tile in range(100):
             rt, lt = half * 20 + tile // 5, tile % 5
-            k = half * TILES + tile
-            fin[k // PIECE, k % PIECE] = frames[8 * rt : 8 * rt + 8, 128 * lt : 128 * lt + 128]
-        for tile in range(100, TILES):
-            k = half * TILES + tile
-            fin[k // PIECE, k % PIECE] = jnp.zeros((8, 128), BF16)
+            fin[half, tile] = frames[8 * rt : 8 * rt + 8, 128 * lt : 128 * lt + 128]
     for h in range(2):
         tail[h, 0:4] = out_in[:, 640 * h : 640 * h + 640]
         tail[h, 4:24] = fc2_in[:, 640 * h : 640 * h + 640]
     for t in range(3):
-        wq[zh, x, zl, c, :, 128 * t : 128 * t + 128] = qkv_in[:, t, :]
-    bias[0:1, :] = b_fc1[...]
+        wq[zh, x, zl, c, :, 128 * t : 128 * t + 128] = qkv_in[t]
+    def flat(ref):
+        return jnp.concatenate([ref[i : i + 1] for i in range(ref.shape[0])], axis=1)
+
+    bias[0:1, :] = flat(b_fc1)
+    for i, ref in enumerate((g1, s1, g2, s2)):
+        norms[i : i + 1] = flat(ref)
     bias[1:2, 0:160] = b_out[...]
     bias[2:3, 0:160] = b_fc2[...]
     bias[3:5, 0:128] = b_qv[...]
-    own_1 = pltpu.make_async_copy(fc1_in, w1.at[zh, x, zl, c], local.at[0])
-    own_1.start()
 
     zq = Ring8(lambda i: wq.at[i // 4, x, lax.rem(i, 4), c], z, at_z, s_zq, r_zq)
     zo = Ring8(lambda i: wo.at[c, y, i // 4, x, lax.rem(i, 4)], z, at_z, s_zo, r_zo)
@@ -212,11 +226,14 @@
     dq = remote(wq.at[:, :, :, c], wq.at[:, :, :, c], s_d.at[0], r_d.at[0], sibling)
     d1 = remote(w1.at[:, :, :, c], w1.at[:, :, :, c], s_d.at[1], r_d.at[1], sibling)
     d2 = remote(w2.at[c], w2.at[c], s_d.at[2], r_d.at[2], sibling)
-    dkv = remote(kv.at[c], kv.at[c], s_d.at[3], r_d.at[3], sibling)
+
+    def dkv(t):
+        return remote(kv.at[c, t], kv.at[c, t], s_kv.at[t], r_kv.at[t], sibling)
+
     do = []
     for n in range(4):
         part = wo.at[c, lax.rem(y + (0, 1, 3, 2)[n], 4)]
-        do.append(remote(part, part, s_d.at[4 + n], r_d.at[4 + n], sibling))
+        do.append(remote(part, part, s_d.at[3 + n], r_d.at[3 + n], sibling))
     bias_sends = []
     for i in range(4):
         for other in range(2):
@@ -237,83 +254,137 @@
     own_b.start()
     own_pair.start()
 
-    def piece_of(x_, zl_, c_):
-        return c_ * 16 + x_ * 4 + zl_
+    def first_tile(x_, zl_):
+        return x_ * 25 + zl_ * PIECE + jnp.minimum(zl_, 1)
 
     def regroup_sends(first, last):
         @pl.loop(first, last)
         def _(i):
             t = lax.rem(clip + i, 32)
             x_, zl_, c_ = t // 8, lax.rem(t // 2, 4), lax.rem(t, 2)
+            tile = first_tile(x_, zl_)
+            device = at(x_=x_, zl_=zl_, c_=c_)
             remote(
-                fin.at[piece_of(x_, zl_, c_)], p1.at[clip], s_p1, r_p1, at(x_=x_, zl_=zl_, c_=c_)
+                fin.at[c_, pl.ds(tile, PIECE)], p1.at[clip, pl.ds(0, PIECE)], s_p1, r_p1, device
             ).start()
 
-    keep_one = pltpu.make_async_copy(fin.at[piece_of(x, zl, c)], p1.at[clip], r_p1)
+            @pl.when(zl_ == 0)
+            def _():
+                remote(
+                    fin.at[c_, tile + PIECE], p1.at[clip, PIECE], s_more, r_more, device
+                ).start()
+
+    own_tile = first_tile(x, zl)
+    keep_one = pltpu.make_async_copy(
+        fin.at[c, pl.ds(own_tile, PIECE)], p1.at[clip, pl.ds(0, PIECE)], r_p1
+    )
     keep_one.start()
-    regroup_sends(1, 9)
+    keep_more = pltpu.make_async_copy(fin.at[c, own_tile + PIECE], p1.at[clip, PIECE], r_more)
+
+    @pl.when(zl == 0)
+    def _():
+        keep_more.start()
+
+    regroup_sends(1, 12)
     own_pair.wait()
     to_pair.wait_recv()
     wo[c, y, zh, x, zl, 0:4] = pair[0, 0:4]
     wo[c, y, zh, x, zl, 4:8] = pair[1, 0:4]
     w2[c, zh, x, zl, 0:20] = pair[0, 4:24]
     w2[c, zh, x, zl, 20:40] = pair[1, 4:24]
-    zo.start(0)
+
+    for i in range(32):
+        keys[i] = servers[i] * 32 + i
+
+    def count_smaller(first, last):
+        @pl.loop(first, last)
+        def _(i):
+            own, total = keys[i], jnp.int32(0)
+            for other in range(32):
+                total = total + jnp.where(keys[other] < own, 1, 0)
+            slots[i] = total
+
+    count_smaller(0, 10)
     zq.relay(0)
-    regroup_sends(9, 17)
-    zo.relay(0)
+    regroup_sends(12, 22)
+    count_smaller(10, 21)
     zq.relay(1)
-    regroup_sends(17, 25)
-    zo.relay(1)
+    regroup_sends(22, 32)
+    x2.start()
+    count_smaller(21, 32)
     zq.relay(2)
-    regroup_sends(25, 32)
-    zo.relay(2)
-    x2.start()
-    for copy in bias_sends:
-        copy.start()
+
+    @pl.loop(0, 32)
+    def _(i):
+        total = jnp.int32(0)
+        for other in range(32):
+            total = total + jnp.where(slots[other] == i, other, 0)
+        order[i] = total
+
+    own_b.wait()
     zq.arrive(3)
     xq.start()
-    own_1.wait()
-    own_b.wait()
-
-    pltpu.make_async_copy(p1, p1, r_p1).wait()
+
+    most = p1.at[:, pl.ds(0, PIECE)]
+    pltpu.make_async_copy(most, most, r_p1).wait()
+
+    @pl.when(zl == 0)
+    def _():
+        pltpu.make_async_copy(p1.at[:, PIECE], p1.at[:, PIECE], r_more).wait()
 
     @pl.loop(0, 32)
     def _(s):
-        p2[s] = p1[order[s]]
+        p2[s, 0:PIECE] = p1[order[s], 0:PIECE]
+
+    @pl.when(zl == 0)
+    def _():
+        @pl.loop(0, 32)
+        def _(s):
+            p2[s, PIECE] = p1[order[s], PIECE]
 
     slot = x * 8 + zl * 2 + zh
-    place = xg.at[y, zh, pl.ds(PIECE * (x * 4 + zl), PIECE)]
+    place = xg.at[y, zh, pl.ds(own_tile, PIECE)]
+    place_more = xg.at[y, zh, own_tile + PIECE]
 
     @pl.loop(1, 32)
     def _(i):
         t = lax.rem(slot + i, 32)
-        remote(
-            p2.at[t], place, s_p2, r_p2, at(x_=t // 8, zl_=lax.rem(t // 2, 4), zh_=lax.rem(t, 2))
-        ).start()
-
-    keep_two = pltpu.make_async_copy(p2.at[slot], place, r_p2)
+        device = at(x_=t // 8, zl_=lax.rem(t // 2, 4), zh_=lax.rem(t, 2))
+        remote(p2.at[t, pl.ds(0, PIECE)], place, s_p2, r_p2, device).start()
+
+        @pl.when(zl == 0)
+        def _():
+            remote(p2.at[t, PIECE], place_more, s_last, r_p2, device).start()
+
+    keep_two = pltpu.make_async_copy(p2.at[slot, pl.ds(0, PIECE)], place, r_p2)
     keep_two.start()
-
+    keep_last = pltpu.make_async_copy(p2.at[slot, PIECE], place_more, r_p2)
+
+    @pl.when(zl == 0)
+    def _():
+        keep_last.start()
+
+    x2.forward()
+    zo.start(0)
     z1.start(0)
-    x2.forward()
-    zo.arrive(3)
-    xo.start()
+    for copy in bias_sends:
+        copy.start()
     xq.forward()
-    xo.forward()
-    x2.arrive()
-    z2.start(0)
+    zo.relay(0)
+    pltpu.make_async_copy(xg.at[y], xg.at[y], r_p2).wait()
+
+    yx(0).start()
+    yx(1).start()
     xq.arrive()
     dq.start()
-    pltpu.make_async_copy(xg.at[y], xg.at[y], r_p2).wait()
-
-    yx(0).start()
-    yx(1).start()
+    zo.relay(1)
     z1.relay(0)
+    yx(0).forward()
+    yx(2).start()
+    zo.relay(2)
     for copy in bias_sends:
         copy.wait_recv()
-    yx(0).forward()
-    yx(2).start()
+    x2.arrive()
     dq.wait_recv()
 
     def project(t):
@@ -336,7 +407,7 @@
                     [block[:, 160 * j : 160 * j + 160] for block in blocks], axis=1
                 )
                 xr[j, pl.ds(start, 16)] = whole
-                xn[j, pl.ds(inner, 16)] = layer_norm(whole.astype(F32), g1[...], s1[...])
+                xn[j, pl.ds(inner, 16)] = layer_norm(whole.astype(F32), norms[0:1], norms[1:2])
 
         left = xn[...].reshape(4 * ROWS, D)
         for h in range(2):
@@ -346,112 +417,104 @@
             query = ((prod[:, 0:128] + biases[3:4, 0:128]) * HDIM ** (-0.5)).astype(BF16)
             key = prod[:, 128:256].astype(BF16)
             value = (prod[:, 256:384] + biases[4:5, 0:128]).astype(BF16)
-            for j in range(4):
-                rows = pl.ds(pl.multiple_of(j * HALF + t * ROWS, 16), ROWS)
-                part = slice(ROWS * j, ROWS * j + ROWS)
-                qs[rows, lanes] = query[part]
-                kv[c, 0, rows, lanes] = key[part]
-                kv[c, 1, rows, lanes] = value[part]
+            qs[t, :, lanes] = query
+            kv[c, t, 0, :, lanes] = key
+            kv[c, t, 1, :, lanes] = value
+        dkv(t).start()
 
     @pl.loop(0, CHUNKS)
     def _(t):
-        @pl.when(t < CHUNKS - 1)
-        def _():
-            yx(t + 1).forward()
-
-        @pl.when(t < CHUNKS - 3)
-        def _():
-            yx(t + 3).start()
-
-        for n in range(3):
-            @pl.when(t == n)
-            def _():
-                z1.relay(n + 1)
-
-        @pl.when(t == 2)
-        def _():
-            z2.relay(0)
-
-        yx(t).arrive()
-        project(t)
-
-    dkv.start()
-    x1.start()
-    xo.arrive()
-    yo.start()
-    do[0].start()
-    z2.relay(1)
-    dkv.wait_recv()
-
-    head_of = lax.broadcasted_iota(jnp.int32, (HALF, 256), 1) // HDIM
-
-    def attend(j):
-        rows = pl.ds(pl.multiple_of(j * HALF, HALF), HALF)
-        q = qs[rows, :]
+        with jax.named_scope("L_fwd"):
+            @pl.when(t < CHUNKS - 1)
+            def _():
+                yx(t + 1).forward()
+
+            @pl.when(t < CHUNKS - 3)
+            def _():
+                yx(t + 3).start()
+
+        with jax.named_scope("L_z1"):
+            @pl.when(t == 0)
+            def _():
+                zo.arrive(3)
+                xo.start()
+                z1.relay(1)
+
+            @pl.when(t == 1)
+            def _():
+                z1.relay(2)
+
+            @pl.when(t == 2)
+            def _():
+                xo.forward()
+                z1.arrive(3)
+                x1.start()
+                z2.start(0)
+
+            @pl.when(t == 4)
+            def _():
+                xo.arrive()
+                yo.start()
+                do[0].start()
+                z2.relay(0)
+
+        with jax.named_scope("L_arr"):
+            yx(t).arrive()
+        with jax.named_scope("L_proj"):
+            project(t)
+
+    for t in range(CHUNKS):
+        dkv(t).wait_recv()
+
+    head_of = lax.broadcasted_iota(jnp.int32, (4 * ROWS, 256), 1) // HDIM
+
+    def rows_of(t):
+        return pl.ds(pl.multiple_of(t * ROWS, ROWS), ROWS)
+
+    def context_send(t, i):
+        j = lax.rem(y + i, 4)
+        n = 3 * t + i - 1
+        return remote(cs.at[t, j], cx.at[y, rows_of(t)], s_cx.at[n], r_cx.at[n], at(y_=j))
+
+    def attend(t):
+        q = qs[t]
         zero = jnp.zeros_like(q)
         stacked = jnp.concatenate([jnp.where(head_of == h, q, zero) for h in range(4)], axis=0)
-        keys = kv[:, 0].reshape(D, 256)
+        keys = kv[:, :, 0].reshape(D, 256)
         scores = lax.dot_general(
             stacked, keys, (((1,), (1,)), ((), ())), preferred_element_type=F32
         )
         weights = jnp.exp(scores - jnp.max(scores, axis=-1, keepdims=True))
         total = jnp.sum(weights, axis=-1, keepdims=True)
-        mixed = dot(weights.astype(BF16), kv[:, 1].reshape(D, 256)) / total
-        context = jnp.zeros((HALF, 256), F32)
+        mixed = dot(weights.astype(BF16), kv[:, :, 1].reshape(D, 256)) / total
+        context = jnp.zeros((4 * ROWS, 256), F32)
         for h in range(4):
-            context = context + jnp.where(head_of == h, mixed[h * HALF : (h + 1) * HALF], 0.0)
-        return context.astype(BF16)
-
-    @pl.loop(1, 4)
-    def _(i):
-        j = lax.rem(y + i, 4)
-        cx[4 + j] = attend(j)
-        remote(cx.at[4 + j], cx.at[y], s_cx.at[i - 1], r_cx.at[i - 1], at(y_=j)).start()
-
-        @pl.when(i == 1)
-        def _():
-            z2.relay(2)
-
-        @pl.when(i == 2)
-        def _():
-            yo.forward()
-            do[1].start()
-            do[2].start()
-
-    x1.forward()
-    z2.arrive(3)
-    d2.start()
-    cx[y] = attend(y)
-    yo.arrive()
-    do[3].start()
-    x1.arrive()
-    d1.start()
-    for i in range(1, 4):
-        remote(cx.at[0], cx.at[0], s_cx.at[i - 1], r_cx.at[i - 1], sibling).wait_recv()
-    for copy in do:
-        copy.wait_recv()
+            part = mixed[h * 4 * ROWS : (h + 1) * 4 * ROWS]
+            context = context + jnp.where(head_of == h, part, 0.0)
+        context = context.astype(BF16)
+        for j in range(4):
+            cs[t, j] = context[j * ROWS : (j + 1) * ROWS]
+        for i in (2, 1, 3):
+            context_send(t, i).start()
+        cx[y, rows_of(t)] = cs[t, y]
 
     def whole_bias(row):
         return jnp.concatenate([bg[h, row : row + 1, 0:160] for h in range(8)], axis=1)
 
-    context = jnp.concatenate([cx[i] for i in range(4)], axis=1)
-    product = jnp.concatenate(
-        [dot(context, wo[h].reshape(1024, 640)) for h in range(2)], axis=1
-    )
-    attended = (xr[y].astype(F32) + whole_bias(1) + product).astype(BF16)
-    att[...] = attended.astype(F32) + whole_bias(2)
-    n2[y] = layer_norm(attended.astype(F32), g2[...], s2[...])
-    yn(0).start()
-    yn(1).start()
-    yn(0).forward()
-    yn(2).start()
-    d1.wait_recv()
-    d2.wait_recv()
+    def attend_out(t):
+        r = rows_of(t)
+        for i in range(1, 4):
+            context_send(t, i).wait_recv()
+        context = jnp.concatenate([cx[i, r] for i in range(4)], axis=1)
+        product = jnp.concatenate(
+            [dot(context, wo[h].reshape(1024, 640)) for h in range(2)], axis=1
+        )
+        attended = (xr[y, r].astype(F32) + whole_bias(1) + product).astype(BF16)
+        att[r] = attended.astype(F32) + whole_bias(2)
+        n2[y, r] = layer_norm(attended.astype(F32), norms[2:3], norms[3:4])
+        yn(t).start()
 
     up, down, far = lax.rem(y + 1, 4), lax.rem(y + 3, 4), lax.rem(y + 2, 4)
-
-    def rows_of(t):
-        return pl.ds(pl.multiple_of(t * ROWS, ROWS), ROWS)
 
     def sums(t):
         r, n = rows_of(t), 4 * t
@@ -514,30 +577,60 @@
         def _():
             remote(fo.at[zh, r], out_rows(t), s_next, r_out, sibling).start()
 
-    @pl.loop(0, CHUNKS)
-    def _(t):
-        @pl.when(t < CHUNKS - 1)
-        def _():
-            yn(t + 1).forward()
-
-        @pl.when(t < CHUNKS - 3)
-        def _():
-            yn(t + 3).start()
-
+    def stage(name, i, lag, work):
+        with jax.named_scope(name):
+            @pl.when((i >= lag) & (i < lag + CHUNKS))
+            def _():
+                work(i - lag)
+
+    def arrived(t):
         yn(t).arrive()
-        feed_forward(t)
-
-        @pl.when(t > 0)
-        def _():
-            add_and_pass(t - 1)
-
-        @pl.when(t > 1)
-        def _():
-            finish(t - 2)
-
-    add_and_pass(CHUNKS - 1)
-    finish(CHUNKS - 2)
-    finish(CHUNKS - 1)
+
+    @pl.loop(0, CHUNKS + 7)
+    def _(i):
+        stage("M_att", i, 0, attend)
+
+        with jax.named_scope("M_w"):
+            @pl.when(i == 0)
+            def _():
+                z2.relay(1)
+
+            @pl.when(i == 1)
+            def _():
+                yo.forward()
+                do[1].start()
+                do[2].start()
+                x1.forward()
+
+            @pl.when(i == 2)
+            def _():
+                z2.relay(2)
+
+            @pl.when(i == 3)
+            def _():
+                yo.arrive()
+                do[3].start()
+                x1.arrive()
+                d1.start()
+                for copy in do:
+                    copy.wait_recv()
+
+            @pl.when(i == 4)
+            def _():
+                z2.arrive(3)
+                d2.start()
+
+            @pl.when(i == 5)
+            def _():
+                d2.wait_recv()
+                d1.wait_recv()
+
+        stage("M_out", i, 3, attend_out)
+        stage("M_fwd", i, 4, lambda t: yn(t).forward())
+        stage("M_arr", i, 5, arrived)
+        stage("M_ff", i, 5, feed_forward)
+        stage("M_add", i, 6, add_and_pass)
+        stage("M_fin", i, 7, finish)
 
     pltpu.make_async_copy(out, out, r_out).wait()
 
@@ -548,51 +641,59 @@
         pltpu.make_async_copy(fo.at[0], fo.at[0], s_next).wait()
 
     to_pair.wait_send()
-    pltpu.make_async_copy(p1.at[pl.ds(0, 31)], p1.at[pl.ds(0, 31)], s_p1).wait()
-    pltpu.make_async_copy(p1.at[pl.ds(0, 31)], p1.at[pl.ds(0, 31)], s_p2).wait()
-    for copy in bias_sends + do + [dq, d1, d2, dkv]:
+    sent = p1.at[pl.ds(0, 31), pl.ds(0, PIECE)]
+    pltpu.make_async_copy(sent, sent, s_p1).wait()
+    pltpu.make_async_copy(sent, sent, s_p2).wait()
+
+    @pl.when(zl == 0)
+    def _():
+        last = p1.at[pl.ds(0, 31), PIECE]
+        pltpu.make_async_copy(last, last, s_last).wait()
+        more = p1.at[pl.ds(0, 7), PIECE]
+        pltpu.make_async_copy(more, more, s_more).wait()
+
+    @pl.when(zl != 0)
+    def _():
+        more = p1.at[pl.ds(0, 8), PIECE]
+        pltpu.make_async_copy(more, more, s_more).wait()
+
+    for copy in bias_sends + do + [dq, d1, d2]:
         copy.wait_send()
-    for i in range(1, 4):
-        remote(cx.at[0], cx.at[0], s_cx.at[i - 1], r_cx.at[i - 1], sibling).wait_send()
     for ring in (zq, zo, z1, z2, xq, xo, x1, x2, yo):
         ring.drain()
 
     @pl.loop(0, CHUNKS)
     def _(t):
         yx(t).drain()
+        dkv(t).wait_send()
         yn(t).drain()
+        for i in range(1, 4):
+            context_send(t, i).wait_send()
         for copy in sums(t):
             copy.wait_send()
-
-
-def slot_order(server_list):
-    clip_count = server_list.shape[0]
-    indices = jnp.arange(clip_count, dtype=jnp.int32)
-    earlier = (server_list[None, :] < server_list[:, None]) | (
-        server_list[None, :] == server_list[:, None]
-    ) & (indices[None, :] < indices[:, None])
-    slot_of = jnp.sum(earlier.astype(jnp.int32), axis=1)
-    return jnp.sum(jnp.where(slot_of[None, :] == indices[:, None], indices[None, :], 0), axis=1)
 
 
 def on_device(
     frames_in, ln1_gain, ln1_bias, qkv_weight, qv_bias, out_weight, out_bias,
     ln2_gain, ln2_bias, fc1_weight, fc1_bias, fc2_weight, fc2_bias, server_of_clip,
 ):
-    clip_order = slot_order(server_of_clip)
-    vmem = pl.BlockSpec(memory_space=pltpu.VMEM)
     smem = pl.BlockSpec(memory_space=pltpu.SMEM)
     dma = pltpu.SemaphoreType.DMA
     V = pltpu.VMEM
     out = pl.pallas_call(
         kernel,
         out_shape=jax.ShapeDtypeStruct((320, 640), BF16),
-        in_specs=[smem] + [vmem] * 13,
-        out_specs=vmem,
+        in_specs=[smem] + [pl.BlockSpec(memory_space=pl.ANY)] * 13,
+        out_specs=pl.BlockSpec(memory_space=pl.ANY),
         scratch_shapes=[
-            V((32, PIECE, 8, 128), BF16),
-            V((32, PIECE, 8, 128), BF16),
-            V((32, PIECE, 8, 128), BF16),
+            pltpu.SMEM((32,), jnp.int32), pltpu.SMEM((32,), jnp.int32), pltpu.SMEM((32,), jnp.int32),
+            V((320, 640), BF16), V((3, 40, 128), BF16), V((4, D), BF16), V((20, D), BF16),
+            V((2, 128), F32), V((1, 160), F32), V((5, 128), F32), V((1, 160), F32),
+            V((10, 128), F32), V((10, 128), F32), V((10, 128), F32), V((10, 128), F32),
+            V((4, D), F32),
+            V((2, TILES, 8, 128), BF16),
+            V((32, PIECE + 1, 8, 128), BF16),
+            V((32, PIECE + 1, 8, 128), BF16),
             V((4, 2, TILES, 8, 128), BF16),
             V((2, 4, 4, 2, 40, 384), BF16),
             V((2, 4, 4, 2, 40, 640), BF16),
@@ -604,9 +705,10 @@
             V((8, 8, 640), F32),
             V((4, HALF, D), BF16),
             V((4, ROWS, D), BF16),
-            V((640, 256), BF16),
-            V((2, 2, 640, 256), BF16),
-            V((8, HALF, 256), BF16),
+            V((CHUNKS, 4 * ROWS, 256), BF16),
+            V((2, CHUNKS, 2, 4 * ROWS, 256), BF16),
+            V((CHUNKS, 4, ROWS, 256), BF16),
+            V((4, HALF, 256), BF16),
             V((HALF, D), F32),
             V((4, HALF, D), BF16),
             V((4, 2, HALF, 640), BF16),
@@ -615,22 +717,23 @@
             V((2, HALF, 640), BF16),
             V((2, HALF, 640), BF16),
             V((2, HALF, 640), BF16),
-            dma((3,)),
-            dma, dma, dma, dma, dma, dma, dma((8,)), dma((8,)),
+            dma((13,)), dma((3,)),
+            dma, dma, dma, dma, dma, dma, dma, dma, dma, dma((8,)), dma((8,)),
             dma((7,)), dma((7,)), dma((7,)), dma((7,)), dma((7,)), dma((7,)), dma((7,)), dma((7,)),
             dma((4,)), dma((4,)), dma((4,)), dma((4,)), dma((4,)), dma((4,)), dma((4,)), dma((4,)),
             dma((4 * CHUNKS,)), dma((4 * CHUNKS,)), dma((4,)), dma((4,)),
             dma((4 * CHUNKS,)), dma((4 * CHUNKS,)),
-            dma((8,)), dma((8,)), dma((3,)), dma((3,)), dma((4 * CHUNKS,)), dma((4 * CHUNKS,)),
+            dma((8,)), dma((8,)), dma((CHUNKS,)), dma((CHUNKS,)), dma((3 * CHUNKS,)), dma((3 * CHUNKS,)), dma((4 * CHUNKS,)), dma((4 * CHUNKS,)),
             dma, dma, dma,
         ],
         compiler_params=pltpu.CompilerParams(
             collective_id=0, has_side_effects=True, vmem_limit_bytes=60 * 2**20
         ),
     )(
-        clip_order, frames_in.reshape(320, 640), qkv_weight, fc1_weight, out_weight, fc2_weight,
-        qv_bias, out_bias[None], fc1_bias[None], fc2_bias[None],
-        ln1_gain[None], ln1_bias[None], ln2_gain[None], ln2_bias[None],
+        server_of_clip, frames_in.reshape(320, 640), qkv_weight.transpose(1, 0, 2), fc1_weight,
+        out_weight, fc2_weight, qv_bias, out_bias[None], fc1_bias.reshape(5, 128), fc2_bias[None],
+        ln1_gain.reshape(10, 128), ln1_bias.reshape(10, 128),
+        ln2_gain.reshape(10, 128), ln2_bias.reshape(10, 128),
     )
     return out.reshape(1, 1, 320, 640)
 

time: 130 us -> 121 us (0.931)
  Pallas kernels: 123 us -> 118 us
  local copies, waits for them, and re-layouts: 5.42 us -> 1.79 us
  other arithmetic: 1.57 us -> 0 us
    pallas_call x1, Pallas kernels: 123 us -> 118 us  [on_device(): pl.pallas_call(kernel, out_shape=jax.ShapeDtypeStruct((320, 640), BF16),...]
    broadcast_in_dim x5 -> x0, local copies, waits for them, and re-layouts: 2.98 us -> none  [the longest x1 0.6 us: on_device(): ln1_gain[None]]
    reduce_sum x2 -> x0, other arithmetic: 1.57 us -> none  [the longest x1 0.91 us: slot_order(): slot_of = jnp.sum(earlier.astype(jnp.int32), axis=1)]
where the time goes in v3:
time: 121 us; the launch traced here: 120 us
  Pallas kernels  118 us (98%)
  local copies, waits for them, and re-layouts  1.79 us (1%)
    pallas_call x1, Pallas kernels, on_device(): pl.pallas_call(kernel, out_shape=jax.ShapeDtypeStruct((320, 640), BF16),...  118 us

profile of v3, /device:TPU:1, one launch (start us, length us, event | category | flops | bytes accessed | tf_op | source)
XLA Modules:
  0.0 120.3 jit_solution(10129354304274519526)
XLA Ops:
  0.0 118.5 %shard_map.136 = bf16[320,640]{1,0:T(8,128)(2,1)} custom-call(s32[32]{0:T(128)} %servers.1, bf16[320,640]{1,0:T(8,128)(2,1)} %bitcast.11, bf16[3,40,128]{2,1,0:T(8,128)(2,1)} %bitcast.12, bf16[40,640]{1,0:T(8,128)(2,1)} %fc1_in.1, bf16[4,1280]{1,0:T(4,128)(2,1)} %out_hbm.1, bf16[20,1280]{1,0:T(8,128)(2,1)} %fc2_hbm.1, f32[2,128]{1,0:T(2,128)} %qv_hbm.1, ...), custom_call_target="tpu_custom_call" | custom-call | tf_op jit(solution)/shard_map/pallas_call | solution.py:683
  118.5 1.8 %copy.16 = bf16[1,1,320,640]{3,2,1,0:T(8,128)(2,1)} copy(bf16[1,1,320,640]{3,2,1,0:T(8,128)(2,1)} %bitcast.10) | data formatting | bytes 819200

commit v4 on v3

--- a/solution.py
+++ b/solution.py
@@ -20,7 +20,8 @@
 D = 1280
 HALF = 160
 TILES = 100
-PIECE = 6
+PART = 3
+FIRST = 16 * PART
 CHUNKS = 5
 ROWS = 32
 
@@ -100,6 +101,36 @@
                 copy.wait_send()
 
 
+class Two8:
+    def __init__(self, slab, i, device, send, recv):
+        def to(block, step, n):
+            return remote(
+                block, block, send.at[n], recv.at[n], device(lax.rem(i + 8 + step, 8))
+            )
+
+        own, low, high = slab(i), slab(lax.rem(i + 6, 8)), slab(lax.rem(i + 2, 8))
+        self.one = [to(own, step, n) for n, step in enumerate((1, -1, 2, -2))]
+        self.two = [to(low, 1, 4), to(high, -1, 5), to(low, 2, 6)]
+
+    def start(self):
+        for copy in self.one:
+            copy.start()
+
+    def forward(self):
+        for copy in self.one:
+            copy.wait_recv()
+        for copy in self.two:
+            copy.start()
+
+    def arrive(self):
+        for copy in self.two:
+            copy.wait_recv()
+
+    def drain(self):
+        for copy in self.one + self.two:
+            copy.wait_send()
+
+
 def layer_norm(floats, gain, shift):
     center = jnp.sum(floats, axis=-1, keepdims=True) * (1.0 / D)
     moved = floats - center
@@ -116,9 +147,9 @@
     g1_hbm, s1_hbm, g2_hbm, s2_hbm,
     out,
     keys, slots, order, frames, qkv_in, out_in, fc2_in, b_qv, b_out, b_fc1, b_fc2, g1, s1, g2, s2,
-    norms, fin, p1, p2, xg, wq, w1, w2, wo, tail, pair, bias, bg, xr, xn, qs, kv, cs, cx, att, n2, pk,
+    norms, fin, p1, pb, pm, p2, xg, wq, w1, w2, wo, tail, pair, bias, bg, xr, xn, qs, kv, cs, cx, att, n2, pk,
     ra, rb, rc, rd, fo,
-    fetch, local, s_p1, r_p1, s_p2, r_p2, s_more, r_more, s_last, s_pair, r_pair, s_bias, r_bias,
+    fetch, local, s_p1, r_p1, s_p2, r_p2, r_b1, r_b2, s_more, r_more, s_last, s_pair, r_pair, s_bias, r_bias,
     s_zq, r_zq, s_zo, r_zo, s_z1, r_z1, s_z2, r_z2,
     s_xq, r_xq, s_xo, r_xo, s_x1, r_x1, s_x2, r_x2,
     s_yx, r_yx, s_yo, r_yo, s_yn, r_yn, s_d, r_d, s_kv, r_kv, s_cx, r_cx, s_rs, r_rs, s_out, s_next, r_out,
@@ -194,9 +225,9 @@
     bias[2:3, 0:160] = b_fc2[...]
     bias[3:5, 0:128] = b_qv[...]
 
-    zq = Ring8(lambda i: wq.at[i // 4, x, lax.rem(i, 4), c], z, at_z, s_zq, r_zq)
-    zo = Ring8(lambda i: wo.at[c, y, i // 4, x, lax.rem(i, 4)], z, at_z, s_zo, r_zo)
-    z1 = Ring8(lambda i: w1.at[i // 4, x, lax.rem(i, 4), c], z, at_z, s_z1, r_z1)
+    zq = Two8(lambda i: wq.at[i // 4, x, lax.rem(i, 4), c], z, at_z, s_zq, r_zq)
+    zo = Two8(lambda i: wo.at[c, y, i // 4, x, lax.rem(i, 4)], z, at_z, s_zo, r_zo)
+    z1 = Two8(lambda i: w1.at[i // 4, x, lax.rem(i, 4), c], z, at_z, s_z1, r_z1)
     z2 = Ring8(lambda i: w2.at[c, i // 4, :, lax.rem(i, 4)], z, at_z, s_z2, r_z2)
     xq = Ring4(lambda i: wq.at[:, i, :, c], lambda i, h: wq.at[h, i, :, c], x, at_x, s_xq, r_xq)
     xo = Ring4(lambda i: wo.at[c, y, :, i], lambda i, h: wo.at[c, y, h, i], x, at_x, s_xo, r_xo)
@@ -250,69 +281,68 @@
     pl.semaphore_wait(barrier, 54)
 
     to_pair.start()
-    zq.start(0)
+    zq.start()
     own_b.start()
     own_pair.start()
 
-    def first_tile(x_, zl_):
-        return x_ * 25 + zl_ * PIECE + jnp.minimum(zl_, 1)
-
-    def regroup_sends(first, last):
+    def tiles_of(x_, zl_, second):
+        if second:
+            return FIRST + x_ * 13 + zl_ * PART + jnp.minimum(zl_, 1)
+        return (x_ * 4 + zl_) * PART
+
+    def regroup_sends(first, last, second):
+        landing, arrived_at = (p1, pb)[second], (r_p1, r_b1)[second]
+
         @pl.loop(first, last)
         def _(i):
             t = lax.rem(clip + i, 32)
             x_, zl_, c_ = t // 8, lax.rem(t // 2, 4), lax.rem(t, 2)
-            tile = first_tile(x_, zl_)
+            tile = tiles_of(x_, zl_, second)
             device = at(x_=x_, zl_=zl_, c_=c_)
             remote(
-                fin.at[c_, pl.ds(tile, PIECE)], p1.at[clip, pl.ds(0, PIECE)], s_p1, r_p1, device
+                fin.at[c_, pl.ds(tile, PART)], landing.at[clip], s_p1, arrived_at, device
             ).start()
-
-            @pl.when(zl_ == 0)
-            def _():
-                remote(
-                    fin.at[c_, tile + PIECE], p1.at[clip, PIECE], s_more, r_more, device
-                ).start()
-
-    own_tile = first_tile(x, zl)
-    keep_one = pltpu.make_async_copy(
-        fin.at[c, pl.ds(own_tile, PIECE)], p1.at[clip, pl.ds(0, PIECE)], r_p1
-    )
-    keep_one.start()
-    keep_more = pltpu.make_async_copy(fin.at[c, own_tile + PIECE], p1.at[clip, PIECE], r_more)
+            if second:
+                @pl.when(zl_ == 0)
+                def _():
+                    remote(
+                        fin.at[c_, tile + PART], pm.at[clip], s_more, r_more, device
+                    ).start()
+
+    own_tiles = [tiles_of(x, zl, second) for second in range(2)]
+    own_more = own_tiles[1] + PART
+    for second in range(2):
+        pltpu.make_async_copy(
+            fin.at[c, pl.ds(own_tiles[second], PART)],
+            (p1, pb)[second].at[clip],
+            (r_p1, r_b1)[second],
+        ).start()
 
     @pl.when(zl == 0)
     def _():
-        keep_more.start()
-
-    regroup_sends(1, 12)
+        pltpu.make_async_copy(fin.at[c, own_more], pm.at[clip], r_more).start()
+
+    regroup_sends(1, 32, 0)
     own_pair.wait()
     to_pair.wait_recv()
     wo[c, y, zh, x, zl, 0:4] = pair[0, 0:4]
     wo[c, y, zh, x, zl, 4:8] = pair[1, 0:4]
     w2[c, zh, x, zl, 0:20] = pair[0, 4:24]
     w2[c, zh, x, zl, 20:40] = pair[1, 4:24]
+    x2.start()
 
     for i in range(32):
         keys[i] = servers[i] * 32 + i
 
-    def count_smaller(first, last):
-        @pl.loop(first, last)
-        def _(i):
-            own, total = keys[i], jnp.int32(0)
-            for other in range(32):
-                total = total + jnp.where(keys[other] < own, 1, 0)
-            slots[i] = total
-
-    count_smaller(0, 10)
-    zq.relay(0)
-    regroup_sends(12, 22)
-    count_smaller(10, 21)
-    zq.relay(1)
-    regroup_sends(22, 32)
-    x2.start()
-    count_smaller(21, 32)
-    zq.relay(2)
+    @pl.loop(0, 32)
+    def _(i):
+        own, total = keys[i], jnp.int32(0)
+        for other in range(32):
+            total = total + jnp.where(keys[other] < own, 1, 0)
+        slots[i] = total
+
+    zq.forward()
+    regroup_sends(1, 32, 1)
 
     @pl.loop(0, 32)
     def _(i):
@@ -322,70 +352,74 @@
         order[i] = total
 
     own_b.wait()
-    zq.arrive(3)
-    xq.start()
-
-    most = p1.at[:, pl.ds(0, PIECE)]
-    pltpu.make_async_copy(most, most, r_p1).wait()
-
-    @pl.when(zl == 0)
-    def _():
-        pltpu.make_async_copy(p1.at[:, PIECE], p1.at[:, PIECE], r_more).wait()
-
-    @pl.loop(0, 32)
-    def _(s):
-        p2[s, 0:PIECE] = p1[order[s], 0:PIECE]
-
-    @pl.when(zl == 0)
-    def _():
+
+    slot = x * 8 + zl * 2 + zh
+
+    def slot_sends(second):
+        part, arrived_at = pl.ds(PART * second, PART), (r_p2, r_b2)[second]
+        landing = (p1, pb)[second]
+        pltpu.make_async_copy(landing, landing, (r_p1, r_b1)[second]).wait()
+
         @pl.loop(0, 32)
         def _(s):
-            p2[s, PIECE] = p1[order[s], PIECE]
-
-    slot = x * 8 + zl * 2 + zh
-    place = xg.at[y, zh, pl.ds(own_tile, PIECE)]
-    place_more = xg.at[y, zh, own_tile + PIECE]
-
-    @pl.loop(1, 32)
-    def _(i):
-        t = lax.rem(slot + i, 32)
-        device = at(x_=t // 8, zl_=lax.rem(t // 2, 4), zh_=lax.rem(t, 2))
-        remote(p2.at[t, pl.ds(0, PIECE)], place, s_p2, r_p2, device).start()
-
-        @pl.when(zl == 0)
-        def _():
-            remote(p2.at[t, PIECE], place_more, s_last, r_p2, device).start()
-
-    keep_two = pltpu.make_async_copy(p2.at[slot, pl.ds(0, PIECE)], place, r_p2)
-    keep_two.start()
-    keep_last = pltpu.make_async_copy(p2.at[slot, PIECE], place_more, r_p2)
-
-    @pl.when(zl == 0)
-    def _():
-        keep_last.start()
-
+            p2[s, part] = landing[order[s]]
+
+        place = xg.at[y, zh, pl.ds(own_tiles[second], PART)]
+        place_more = xg.at[y, zh, own_more]
+        if second:
+            @pl.when(zl == 0)
+            def _():
+                pltpu.make_async_copy(pm, pm, r_more).wait()
+
+                @pl.loop(0, 32)
+                def _(s):
+                    p2[s, 2 * PART] = pm[order[s]]
+
+        @pl.loop(1, 32)
+        def _(i):
+            t = lax.rem(slot + i, 32)
+            device = at(x_=t // 8, zl_=lax.rem(t // 2, 4), zh_=lax.rem(t, 2))
+            remote(p2.at[t, part], place, s_p2, arrived_at, device).start()
+            if second:
+                @pl.when(zl == 0)
+                def _():
+                    remote(p2.at[t, 2 * PART], place_more, s_last, arrived_at, device).start()
+
+        pltpu.make_async_copy(p2.at[slot, part], place, arrived_at).start()
+        if second:
+            @pl.when(zl == 0)
+            def _():
+                pltpu.make_async_copy(p2.at[slot, 2 * PART], place_more, arrived_at).start()
+
+    slot_sends(0)
+    zo.start()
+    zq.arrive()
+    xq.start()
+    slot_sends(1)
     x2.forward()
-    zo.start(0)
-    z1.start(0)
     for copy in bias_sends:
         copy.start()
-    xq.forward()
-    zo.relay(0)
-    pltpu.make_async_copy(xg.at[y], xg.at[y], r_p2).wait()
-
+    here = xg.at[y, :, pl.ds(0, FIRST)]
+    pltpu.make_async_copy(here, here, r_p2).wait()
     yx(0).start()
     yx(1).start()
+    zo.forward()
+    z1.start()
+    xq.forward()
+    yx(0).forward()
+    x2.arrive()
+    here = xg.at[y, :, pl.ds(FIRST, TILES - FIRST)]
+    pltpu.make_async_copy(here, here, r_b2).wait()
+    yx(2).start()
+    yx(1).forward()
+    yx(3).start()
     xq.arrive()
     dq.start()
-    zo.relay(1)
-    z1.relay(0)
-    yx(0).forward()
-    yx(2).start()
-    zo.relay(2)
     for copy in bias_sends:
         copy.wait_recv()
-    x2.arrive()
     dq.wait_recv()
+    zo.arrive()
+    xo.start()
 
     def project(t):
         @pl.loop(0, 2)
@@ -425,44 +459,41 @@
     @pl.loop(0, CHUNKS)
     def _(t):
         with jax.named_scope("L_fwd"):
-            @pl.when(t < CHUNKS - 1)
-            def _():
-                yx(t + 1).forward()
-
-            @pl.when(t < CHUNKS - 3)
-            def _():
-                yx(t + 3).start()
+            @pl.when(t < CHUNKS - 2)
+            def _():
+                yx(t + 2).forward()
+
+            @pl.when(t < CHUNKS - 4)
+            def _():
+                yx(t + 4).start()
 
         with jax.named_scope("L_z1"):
             @pl.when(t == 0)
             def _():
-                zo.arrive(3)
-                xo.start()
-                z1.relay(1)
+                z1.forward()
+                z2.start(0)
 
             @pl.when(t == 1)
             def _():
-                z1.relay(2)
+                xo.forward()
 
             @pl.when(t == 2)
             def _():
-                xo.forward()
-                z1.arrive(3)
+                z1.arrive()
                 x1.start()
-                z2.start(0)
-
-            @pl.when(t == 4)
+
+            @pl.when(t == 3)
             def _():
                 xo.arrive()
                 yo.start()
                 do[0].start()
-                z2.relay(0)
 
         with jax.named_scope("L_arr"):
             yx(t).arrive()
         with jax.named_scope("L_proj"):
             project(t)
 
+    z2.relay(0)
     for t in range(CHUNKS):
         dkv(t).wait_recv()
 
@@ -533,6 +564,11 @@
             total = dot(left, w1[h].reshape(D, 640)) + bg[y * 2 + h, 0:1, :]
             parts.append((0.5 * total * (1.0 + lax.erf(total * 0.5**0.5))).astype(BF16))
         hidden = jnp.concatenate(parts, axis=1)
+
+        @pl.when(t == 0)
+        def _():
+            d2.wait_recv()
+
         share = jnp.concatenate(
             [dot(hidden, w2[h].reshape(D, 640)) for h in range(2)], axis=1
         )
@@ -577,60 +613,74 @@
         def _():
             remote(fo.at[zh, r], out_rows(t), s_next, r_out, sibling).start()
 
-    def stage(name, i, lag, work):
-        with jax.named_scope(name):
-            @pl.when((i >= lag) & (i < lag + CHUNKS))
-            def _():
-                work(i - lag)
-
-    def arrived(t):
-        yn(t).arrive()
-
-    @pl.loop(0, CHUNKS + 7)
-    def _(i):
-        stage("M_att", i, 0, attend)
+    @pl.loop(0, CHUNKS)
+    def _(t):
+        with jax.named_scope("M_att"):
+            attend(t)
 
         with jax.named_scope("M_w"):
-            @pl.when(i == 0)
-            def _():
-                z2.relay(1)
-
-            @pl.when(i == 1)
+            @pl.when(t == 1)
             def _():
                 yo.forward()
                 do[1].start()
                 do[2].start()
+
+            @pl.when(t == 2)
+            def _():
                 x1.forward()
-
-            @pl.when(i == 2)
+                z2.relay(1)
+
+    yo.arrive()
+    do[3].start()
+    for copy in do:
+        copy.wait_recv()
+
+    @pl.loop(0, CHUNKS)
+    def _(t):
+        with jax.named_scope("O_out"):
+            attend_out(t)
+
+        with jax.named_scope("O_z2"):
+            @pl.when(t == 0)
             def _():
                 z2.relay(2)
-
-            @pl.when(i == 3)
-            def _():
-                yo.arrive()
-                do[3].start()
                 x1.arrive()
                 d1.start()
-                for copy in do:
-                    copy.wait_recv()
-
-            @pl.when(i == 4)
+
+            @pl.when(t == CHUNKS - 1)
             def _():
                 z2.arrive(3)
                 d2.start()
 
-            @pl.when(i == 5)
-            def _():
-                d2.wait_recv()
-                d1.wait_recv()
-
-        stage("M_out", i, 3, attend_out)
-        stage("M_fwd", i, 4, lambda t: yn(t).forward())
-        stage("M_arr", i, 5, arrived)
-        stage("M_ff", i, 5, feed_forward)
-        stage("M_add", i, 6, add_and_pass)
-        stage("M_fin", i, 7, finish)
+        with jax.named_scope("O_fwd"):
+            @pl.when(t > 1)
+            def _():
+                yn(t - 2).forward()
+
+    d1.wait_recv()
+
+    @pl.loop(0, CHUNKS + 2)
+    def _(i):
+        @pl.when(i < CHUNKS)
+        def _():
+            with jax.named_scope("M_arr"):
+                yn(i).arrive()
+            with jax.named_scope("M_ff"):
+                feed_forward(i)
+            with jax.named_scope("M_fwd"):
+                @pl.when(i < 2)
+                def _():
+                    yn(i + 3).forward()
+
+        with jax.named_scope("M_add"):
+            @pl.when((i > 0) & (i <= CHUNKS))
+            def _():
+                add_and_pass(i - 1)
+
+        with jax.named_scope("M_fin"):
+            @pl.when(i > 1)
+            def _():
+                finish(i - 2)
 
     pltpu.make_async_copy(out, out, r_out).wait()
 
@@ -641,20 +691,20 @@
         pltpu.make_async_copy(fo.at[0], fo.at[0], s_next).wait()
 
     to_pair.wait_send()
-    sent = p1.at[pl.ds(0, 31), pl.ds(0, PIECE)]
+    sent = p2.at[pl.ds(0, 31), pl.ds(0, 2 * PART)]
     pltpu.make_async_copy(sent, sent, s_p1).wait()
     pltpu.make_async_copy(sent, sent, s_p2).wait()
 
     @pl.when(zl == 0)
     def _():
-        last = p1.at[pl.ds(0, 31), PIECE]
+        last = p2.at[pl.ds(0, 31), 2 * PART]
         pltpu.make_async_copy(last, last, s_last).wait()
-        more = p1.at[pl.ds(0, 7), PIECE]
+        more = pm.at[pl.ds(0, 7)]
         pltpu.make_async_copy(more, more, s_more).wait()
 
     @pl.when(zl != 0)
     def _():
-        more = p1.at[pl.ds(0, 8), PIECE]
+        more = pm.at[pl.ds(0, 8)]
         pltpu.make_async_copy(more, more, s_more).wait()
 
     for copy in bias_sends + do + [dq, d1, d2]:
@@ -692,8 +742,10 @@
             V((10, 128), F32), V((10, 128), F32), V((10, 128), F32), V((10, 128), F32),
             V((4, D), F32),
             V((2, TILES, 8, 128), BF16),
-            V((32, PIECE + 1, 8, 128), BF16),
-            V((32, PIECE + 1, 8, 128), BF16),
+            V((32, PART, 8, 128), BF16),
+            V((32, PART, 8, 128), BF16),
+            V((32, 8, 128), BF16),
+            V((32, 2 * PART + 1, 8, 128), BF16),
             V((4, 2, TILES, 8, 128), BF16),
             V((2, 4, 4, 2, 40, 384), BF16),
             V((2, 4, 4, 2, 40, 640), BF16),
@@ -718,7 +770,7 @@
             V((2, HALF, 640), BF16),
             V((2, HALF, 640), BF16),
             dma((13,)), dma((3,)),
-            dma, dma, dma, dma, dma, dma, dma, dma, dma, dma((8,)), dma((8,)),
+            dma, dma, dma, dma, dma, dma, dma, dma, dma, dma, dma, dma((8,)), dma((8,)),
             dma((7,)), dma((7,)), dma((7,)), dma((7,)), dma((7,)), dma((7,)), dma((7,)), dma((7,)),
             dma((4,)), dma((4,)), dma((4,)), dma((4,)), dma((4,)), dma((4,)), dma((4,)), dma((4,)),
             dma((4 * CHUNKS,)), dma((4 * CHUNKS,)), dma((4,)), dma((4,)),

time: 121 us -> 110 us (0.909)
  Pallas kernels: 118 us -> 108 us
    pallas_call x1, Pallas kernels: 118 us -> 108 us  [on_device(): pl.pallas_call(kernel, out_shape=jax.ShapeDtypeStruct((320, 640), BF16),...]
where the time goes in v4:
time: 110 us
  Pallas kernels  108 us (98%)
  local copies, waits for them, and re-layouts  1.79 us (2%)
    pallas_call x1, Pallas kernels, on_device(): pl.pallas_call(kernel, out_shape=jax.ShapeDtypeStruct((320, 640), BF16),...  108 us

profile of v4, /device:TPU:1, one launch (start us, length us, event | category | flops | bytes accessed | tf_op | source)
XLA Modules:
  0.0 109.9 jit_solution(11898438935012523772)
XLA Ops:
  0.0 108.1 %shard_map.136 = bf16[320,640]{1,0:T(8,128)(2,1)} custom-call(s32[32]{0:T(128)} %servers.1, bf16[320,640]{1,0:T(8,128)(2,1)} %bitcast.11, bf16[3,40,128]{2,1,0:T(8,128)(2,1)} %bitcast.12, bf16[40,640]{1,0:T(8,128)(2,1)} %fc1_in.1, bf16[4,1280]{1,0:T(4,128)(2,1)} %out_hbm.1, bf16[20,1280]{1,0:T(8,128)(2,1)} %fc2_hbm.1, f32[2,128]{1,0:T(2,128)} %qv_hbm.1, ...), custom_call_target="tpu_custom_call" | custom-call | tf_op jit(solution)/shard_map/pallas_call | solution.py:733
  108.1 1.8 %copy.16 = bf16[1,1,320,640]{3,2,1,0:T(8,128)(2,1)} copy(bf16[1,1,320,640]{3,2,1,0:T(8,128)(2,1)} %bitcast.10) | data formatting | bytes 819200

commit v5 on v4

--- a/solution.py
+++ b/solution.py
@@ -341,8 +341,9 @@
             total = total + jnp.where(keys[other] < own, 1, 0)
         slots[i] = total
 
+    regroup_sends(1, 11, 1)
     zq.forward()
-    regroup_sends(1, 32, 1)
+    regroup_sends(11, 32, 1)
 
     @pl.loop(0, 32)
     def _(i):

time: 110 us -> 110 us (level)
  no operation moved by 1% of the time
where the time goes in v5:
time: 110 us
  Pallas kernels  108 us (98%)
  local copies, waits for them, and re-layouts  1.79 us (2%)
    pallas_call x1, Pallas kernels, on_device(): pl.pallas_call(kernel, out_shape=jax.ShapeDtypeStruct((320, 640), BF16),...  108 us

profile of v5, /device:TPU:1, one launch (start us, length us, event | category | flops | bytes accessed | tf_op | source)
XLA Modules:
  0.0 110.2 jit_solution(14248069886110597326)
XLA Ops:
  0.0 108.4 %shard_map.136 = bf16[320,640]{1,0:T(8,128)(2,1)} custom-call(s32[32]{0:T(128)} %servers.1, bf16[320,640]{1,0:T(8,128)(2,1)} %bitcast.11, bf16[3,40,128]{2,1,0:T(8,128)(2,1)} %bitcast.12, bf16[40,640]{1,0:T(8,128)(2,1)} %fc1_in.1, bf16[4,1280]{1,0:T(4,128)(2,1)} %out_hbm.1, bf16[20,1280]{1,0:T(8,128)(2,1)} %fc2_hbm.1, f32[2,128]{1,0:T(2,128)} %qv_hbm.1, ...), custom_call_target="tpu_custom_call" | custom-call | tf_op jit(solution)/shard_map/pallas_call | solution.py:734
  108.4 1.8 %copy.16 = bf16[1,1,320,640]{3,2,1,0:T(8,128)(2,1)} copy(bf16[1,1,320,640]{3,2,1,0:T(8,128)(2,1)} %bitcast.10) | data formatting | bytes 819200
